TPU v7x, 32 devices: a whole 2x2x4 slice. The times are simulated.
32 devices in a mesh: wall: 8 (over y, x, core), span: 4 (over z).
Axes of the slice: x: 2, y: 2, z: 4, core: 2. Of those that a mesh axis runs over, the one named last changes fastest.
Arguments:
- velocity_old: float32 [3, 128, 64, 128], P(None, 'wall', 'span'), may hold values from -12 to 12, as said below
- heights: float32 [16], replicated, may hold values from 0.04 to 0.25
- owner_device: int32 [16384, 1], P(('wall', 'span')), may hold values from 0 to 7, as said below
- owner_element: int32 [16384, 1], P(('wall', 'span')), may hold values from 0 to 63, as said below
- ref_coords: float32 [3, 16384], P(None, ('wall', 'span')), may hold values from -1 to 1
- roughness: float32 [16384], P(('wall', 'span')), may hold values from 0.0001 to 0.01
Outputs:
- velocity_new: float32 [3, 128, 64, 128], P(None, 'wall', 'span')
- neumann: float32 [2, 16384], P(None, ('wall', 'span'))
Inputs may be any that keep to these rules, and one draw needn't show every extreme that they name: `velocity_old`: values at coinciding nodes of neighbouring elements are equal. `owner_device`: the owner is the streamwise index w of the point's own device, or w + 1 or w - 1 modulo 8. Among the rows of one device at most 128 name w + 1 and at most 128 name w - 1; some device has exactly 128 for w + 1 and some device exactly 128 for w - 1. `owner_element`: the element index is (ex * 2 + ez) * 16 + ey with ex = i // 8 and ez = j // 8 of the wall point; ey < 2 for points of the first wall, ey >= 14 for the second.
All inputs are finite; a program needn't handle non-finite values.
Results may differ from a plain program's by a relative error of at most 0.0003.
Values sent between devices are 32-bit elements; how exact they have to be, the bound alone decides.
A program may use at most 128 MiB of HBM per device.

v0:
```python
import functools

import jax
import jax.numpy as jnp
import numpy as np
from jax import lax
from jax.experimental import pallas as pl
from jax.experimental.pallas import tpu as pltpu
from jax.sharding import PartitionSpec as P

GLL_NODES = (
    -1.0,
    -0.8717401485096066,
    -0.5917001814331423,
    -0.2092992179024789,
    0.2092992179024789,
    0.5917001814331423,
    0.8717401485096066,
    1.0,
)
GLL_WEIGHTS = (
    0.03571428571428571,
    0.2107042271435061,
    0.3411226924835044,
    0.4124587946587038,
    0.4124587946587038,
    0.3411226924835044,
    0.2107042271435061,
    0.03571428571428571,
)
viscosity = 0.02
inverse_step = 20.0
karman = 0.41
sample_height = 0.1
speed_floor = 0.01
element_dx = 0.05
element_dz = 0.13
NEAR = 2
ROUNDS = 2
REACH = 2
TERMS = (
    (0, 0, 0),
    (1, 1, 2),
    (1, 2, 1),
    (2, 2, 2),
    (3, 3, 6),
    (3, 4, 5),
    (3, 5, 4),
    (3, 6, 3),
    (4, 4, 6),
    (4, 6, 4),
    (5, 5, 6),
    (5, 6, 5),
    (6, 6, 6),
)
SINGLE_STAGE = 64
MESH = pl.DeviceIdType.MESH
F32 = jnp.float32
BF16 = jnp.bfloat16


def stiffness_table():
    points = np.array(GLL_NODES)
    weights = np.array(GLL_WEIGHTS)
    previous = np.ones(8)
    current = points.copy()
    for degree in range(1, 7):
        previous, current = (
            current,
            ((2 * degree + 1) * points * current - degree * previous) / (degree + 1),
        )
    derivative = np.zeros((8, 8))
    for target in range(8):
        for source in range(8):
            if target != source:
                derivative[target, source] = (
                    current[target] / current[source] / (points[target] - points[source])
                )
    derivative[0, 0] = -14.0
    derivative[7, 7] = 14.0
    return derivative.T @ (weights[:, None] * derivative)


def join_matrix(length):
    joined = np.eye(length)
    for left in range(7, length - 1, 8):
        joined[left, left + 1] = 1.0
        joined[left + 1, left] = 1.0
    return joined


def face_weights(length, open_ends):
    values = np.ones(length)
    position = np.arange(length) % 8
    values[(position == 0) | (position == 7)] = 0.5
    if open_ends:
        values[0] = 1.0
        values[-1] = 1.0
    return values


def split_np(matrix):
    single = jnp.asarray(matrix, F32)
    high = single.astype(BF16)
    low = (jnp.asarray(matrix, F32) - high.astype(F32)).astype(BF16)
    return high, low


def tables(length_x, length_z, length_y):
    weights = np.array(GLL_WEIGHTS)
    stiffness = stiffness_table()
    count_x, count_z, count_y = length_x // 8, length_z // 8, length_y // 8
    mass_x = np.tile(0.5 * element_dx * weights, count_x)
    mass_z = np.tile(0.5 * element_dz * weights, count_z)
    stiff_x = np.kron(np.eye(count_x), stiffness * (2.0 / element_dx))
    stiff_z = np.kron(np.eye(count_z), stiffness * (2.0 / element_dz))
    mass_xz = np.kron(mass_x, mass_z)
    join_xz = np.kron(join_matrix(length_x), join_matrix(length_z))
    join_y = join_matrix(length_y)
    plane = viscosity * (
        np.kron(stiff_x, np.diag(mass_z)) + np.kron(np.diag(mass_x), stiff_z)
    ) + inverse_step * np.diag(mass_xz)
    plane = join_xz @ plane
    mass_plane = join_xz @ np.diag(mass_xz)
    both = np.concatenate([plane, mass_plane], axis=1)
    lines_mass = np.tile(0.5 * weights, count_y)[:, None] * join_y
    lines_stiff = viscosity * 2.0 * (np.kron(np.eye(count_y), stiffness) @ join_y)
    lines = np.stack([lines_mass, lines_stiff])
    ring_x = join_matrix(length_x) @ mass_x
    ring_z = join_matrix(length_z) @ mass_z
    ring_x[0] *= 2.0
    ring_x[-1] *= 2.0
    ring_z[0] *= 2.0
    ring_z[-1] *= 2.0
    assembled = inverse_step * np.kron(ring_x, ring_z)
    inner_x = face_weights(length_x, True)
    inner_z = face_weights(length_z, True)
    outer_x = face_weights(length_x, False)
    outer_z = face_weights(length_z, False)
    weight_y = face_weights(length_y, True)
    columns = np.stack(
        [
            assembled[:, None] * np.ones(length_y)[None],
            np.kron(outer_x, outer_z)[:, None] * weight_y[None],
            np.kron(inner_x, inner_z)[:, None] * weight_y[None],
        ]
    )
    reach = 2 * REACH + 1

    def words(length, mass, stiff, extra):
        size = reach * length
        join = join_matrix(size)
        light = join @ np.diag(np.tile(mass, reach))
        heavy = viscosity * join @ np.kron(np.eye(size // 8), stiff) + extra * light
        chains = [
            light,
            heavy @ light,
            light @ light,
            heavy @ heavy @ light,
            heavy @ light @ light,
            light @ heavy @ light,
            light @ light @ light,
        ]
        middle = REACH * length
        chains = [chain[middle : middle + length] for chain in chains]
        return np.concatenate(chains + [np.zeros((128 - 7 * length, size))], axis=0)

    words_x = words(length_x, mass_x, stiffness * (2.0 / element_dx), 0.0)
    words_z = words(length_z, mass_z, stiffness * (2.0 / element_dz), inverse_step)
    pad = np.zeros((128, 128 - reach * length_z))
    words_z = np.concatenate([words_z, pad], axis=1)
    return both, lines, columns, words_x, words_z


def split(value):
    high = value.astype(BF16)
    low = (value - high.astype(F32)).astype(BF16)
    return high, low


def dot3(left, right, dims):
    def one(a, b):
        return lax.dot_general(a, b, (dims, ((), ())), preferred_element_type=F32)

    return one(left[0], right[0]) + (one(left[0], right[1]) + one(left[1], right[0]))


NN = ((1,), (0,))
NT = ((1,), (1,))
TN = ((0,), (0,))
DIRS = ((1, 1), (1, -1), (-1, 1), (-1, -1))


def lagrange_rows(coord):
    points = np.array(GLL_NODES)
    scale = 1.0 / np.prod(points[:, None] - points[None, :] + np.eye(8), axis=1)
    shape = (8, coord.shape[1])
    node = lax.broadcasted_iota(jnp.int32, shape, 0)
    total = jnp.zeros(shape, F32)
    for a in range(8):
        total = jnp.where(node == a, F32(scale[a]), total)
    for b in range(8):
        total = total * jnp.where(node == b, F32(1.0), coord - F32(points[b]))
    return total


def kernel(
    n_wall,
    n_span,
    sizes,
    vel_in,
    heights_in,
    owner_in,
    element_in,
    coords_in,
    roughness_in,
    plane_hi_in,
    plane_lo_in,
    lines_in,
    columns_in,
    words_x_in,
    words_z_in,
    out,
    neumann,
    vel,
    heights,
    owner,
    element,
    coords,
    roughness,
    plane_hi,
    plane_lo,
    lines,
    columns,
    words_x,
    words_z,
    load_sem,
    near,
    near_got,
    field,
    local,
    z_send,
    c_send,
    x_got,
    z_got,
    c_got,
    parts,
    sum_send,
    wall_got,
    span_got,
    pull_send,
    pull_got,
    pull_ss,
    pull_rs,
    near_ss,
    near_rs,
    face_ss,
    face_rs,
    wall_ss,
    wall_rs,
    span_ss,
    span_rs,
):
    length_x, length_z, length_y = sizes
    rows = length_x * length_z
    count_z, count_y = length_z // 8, length_y // 8
    w = lax.axis_index("wall")
    s = lax.axis_index("span")

    def at(dx, dz):
        return (lax.rem(w + (dx + n_wall), n_wall), lax.rem(s + (dz + n_span), n_span))

    loads = [
        pltpu.make_async_copy(source, target, load_sem.at[index])
        for index, (source, target) in enumerate(
            (
                (vel_in, vel),
                (heights_in, heights),
                (lines_in, lines),
                (coords_in, coords),
                (owner_in, owner),
                (element_in, element),
                (columns_in, columns),
                (roughness_in, roughness),
                (plane_hi_in, plane_hi),
                (plane_lo_in, plane_lo),
                (words_x_in, words_x),
                (words_z_in, words_z),
            )
        )
    ]
    for load in loads:
        load.start()

    single = n_wall * n_span <= SINGLE_STAGE
    if single:
        greeted = [divmod(k, n_span) for k in range(1, n_wall * n_span)]
    else:
        greeted = [(k, 0) for k in range(1, n_wall)] + [(0, k) for k in range(1, n_span)]
        greeted += sorted(
            {
                ((dx + n_wall) % n_wall, (dz + n_span) % n_span)
                for dx in range(-REACH, REACH + 1)
                for dz in range(-REACH, REACH + 1)
            }
            - {(0, 0)}
            - set(greeted)
        )
    barrier = pltpu.get_barrier_semaphore()
    for dx, dz in greeted:
        pl.semaphore_signal(barrier, inc=1, device_id=at(dx, dz), device_id_type=MESH)

    loads[0].wait()
    lane = lax.broadcasted_iota(jnp.int32, (64, length_y), 1)
    groups = (length_x // 8) * count_z
    for index, comp in enumerate((0, 2)):
        packed = jnp.zeros((64, length_y), F32)
        for group in range(groups):
            ex, ez = group // count_z, group % count_z
            block = vel[comp, pl.ds(ex * 8, 8), pl.ds(ez * 8, 8), :].reshape(64, length_y)
            moved = pltpu.roll(block, (group * 32 + 16) % length_y, 1)
            packed = jnp.where(lane // 32 == group, moved, packed)
        near[index] = packed
    for load in loads[1:]:
        load.wait()

    layer_of = lax.broadcasted_iota(jnp.int32, (length_y, count_y), 0) // 8
    layer = lax.broadcasted_iota(jnp.int32, (length_y, count_y), 1)
    height_row = heights[...]
    height = jnp.sum(jnp.where(layer_of == layer, height_row, 0.0), axis=1, keepdims=True)
    lines_mass = height * lines[0]
    lines_hi, lines_lo = split(jnp.concatenate([lines_mass, lines[1] / height], axis=1))
    bound = jnp.max(0.1535 * height_row + 0.000182 / height_row, axis=1, keepdims=True)
    shifts = (0.15 * bound, 0.85 * bound)

    mass_row = jnp.sum(lines_mass, axis=0, keepdims=True)
    scale = columns[0] * mass_row
    for c in range(3):
        field[0, c] = vel[c].reshape(rows, length_y) * scale

    def remote(src, dst, ss, rs, where):
        return pltpu.make_async_remote_copy(
            src_ref=src,
            dst_ref=dst,
            send_sem=ss,
            recv_sem=rs,
            device_id=where,
            device_id_type=MESH,
        )

    def face_copies(turn):
        copies = []
        for slot, dx in enumerate((1, -1)):
            start = rows - length_z if dx == 1 else 0
            copies.append(
                remote(
                    local.at[turn, :, pl.ds(start, length_z), :],
                    x_got.at[turn, slot],
                    face_ss.at[turn, slot],
                    face_rs.at[turn, slot],
                    at(dx, 0),
                )
            )
        for slot, dz in enumerate((1, -1)):
            copies.append(
                remote(
                    z_send.at[turn, slot],
                    z_got.at[turn, slot],
                    face_ss.at[turn, 2 + slot],
                    face_rs.at[turn, 2 + slot],
                    at(0, dz),
                )
            )
        for slot, (dx, dz) in enumerate(DIRS):
            copies.append(
                remote(
                    c_send.at[turn, slot, pl.ds(0, 3), :],
                    c_got.at[turn, slot, pl.ds(0, 3), :],
                    face_ss.at[turn, 4 + slot],
                    face_rs.at[turn, 4 + slot],
                    at(dx, dz),
                )
            )
        return copies

    def corner(dx, dz):
        return (rows - length_z if dx == 1 else 0) + (length_z - 1 if dz == 1 else 0)

    def send_faces(turn):
        for c in range(3):
            for slot, dz in enumerate((1, -1)):
                edge = length_z - 1 if dz == 1 else 0
                z_send[turn, slot, c] = local[turn, c, pl.ds(edge, length_x, stride=length_z), :]
            for slot, (dx, dz) in enumerate(DIRS):
                at_row = corner(dx, dz)
                c_send[turn, slot, c : c + 1, :] = local[turn, c, at_row : at_row + 1, :]
        if turn == 0:
            pl.semaphore_wait(barrier, len(greeted))
            for copy in near_copies:
                copy.start()
        copies = face_copies(turn)
        for copy in copies:
            copy.start()
        return copies

    def add_faces(turn, copies):
        for copy in copies:
            copy.wait()
        for c in range(3):
            for slot, dx in enumerate((1, -1)):
                start = 0 if dx == 1 else rows - length_z
                field[turn + 1, c, pl.ds(start, length_z), :] += x_got[turn, slot, c]
            for slot, dz in enumerate((1, -1)):
                edge = pl.ds(0 if dz == 1 else length_z - 1, length_x, stride=length_z)
                field[turn + 1, c, edge, :] = field[turn + 1, c, edge, :] + z_got[turn, slot, c]
            for slot, (dx, dz) in enumerate(DIRS):
                at_row = corner(-dx, -dz)
                field[turn + 1, c, at_row : at_row + 1, :] += c_got[turn, slot, c : c + 1, :]

    def inner(quantity, c, product):
        parts[quantity * 8 + c : quantity * 8 + c + 1, :] = jnp.sum(
            product, axis=0, keepdims=True
        )

    def operate(source, target):
        flat = field[source].reshape(3 * rows, length_y)
        lined = dot3(split(flat), (lines_hi, lines_lo), NN)
        wide = jnp.concatenate(
            [
                jnp.concatenate(
                    [
                        lined[c * rows : (c + 1) * rows, :length_y],
                        lined[c * rows : (c + 1) * rows, length_y:],
                    ],
                    axis=0,
                )
                for c in range(3)
            ],
            axis=1,
        )
        result = dot3((plane_hi[...], plane_lo[...]), split(wide), NN)
        for c in range(3):
            local[target, c] = result[:, c * length_y : (c + 1) * length_y]

    slots = {(0, 0): 0, (0, 1): 1, (1, 1): 2, (0, 2): 3, (1, 2): 4, (2, 2): 5}

    def inner_products(newest):
        for c in range(3):
            weighted = field[newest, c] * columns[1]
            for other in range(newest + 1):
                inner(slots[(other, newest)], c, weighted * field[other, c])

    near_copies = []
    for slot, dx in enumerate((1, -1)):
        copy = remote(near, near_got.at[slot], near_ss.at[slot], near_rs.at[slot], at(dx, 0))
        near_copies.append(copy)

    operate(0, 0)
    copies_one = send_faces(0)
    for c in range(3):
        field[1, c] = local[0, c]
    parts[...] = jnp.zeros_like(parts)

    points = owner.shape[1]
    row_x = lagrange_rows(coords[0:1, :])
    row_z = lagrange_rows(coords[1:2, :])
    row_y = lagrange_rows(coords[2:3, :])
    cross = jnp.concatenate([row_x[a : a + 1] * row_z for a in range(8)], axis=0)
    distance = lax.rem(owner[...] - w + n_wall, n_wall)
    from_next = distance == 1
    from_prev = distance == n_wall - 1
    own = jnp.logical_not(jnp.logical_or(from_next, from_prev))
    spread = jnp.concatenate(
        [jnp.where(mask, cross, 0.0) for mask in (own, from_prev, from_next)], axis=0
    )
    n_row = lax.broadcasted_iota(jnp.int32, (length_y, points), 0)
    within = (n_row % 32) // 8
    layer_y = jnp.where(within < NEAR, within + (count_y - NEAR), within - NEAR)
    wanted = (n_row // 32) * count_y + layer_y == element[...]
    along = jnp.where(wanted, jnp.concatenate([row_y] * (length_y // 8), axis=0), 0.0)
    spread = split(spread)

    for copy in near_copies:
        copy.wait()

    sampled = []
    for index in range(2):
        sources = jnp.concatenate(
            [near[index], near_got[0, index], near_got[1, index]], axis=0
        )
        values = dot3(split(sources), spread, TN)
        sampled.append(jnp.sum(values * along, axis=0, keepdims=True))
    stream, spanwise = sampled
    speed = jnp.sqrt(stream * stream + spanwise * spanwise + speed_floor)
    drag = karman / jnp.log(sample_height / roughness[...])
    factor = -(drag * drag * speed / viscosity)
    gradient = (factor * stream, factor * spanwise)
    neumann[0:1, :] = gradient[0]
    neumann[1:2, :] = gradient[1]

    planes = []
    for index in range(2):
        pull = viscosity * gradient[index]
        planes += [pull[:, :rows], pull[:, rows:]]
    node = lax.broadcasted_iota(jnp.int32, (length_x, rows), 1) // length_z
    node_row = lax.broadcasted_iota(jnp.int32, (length_x, rows), 0)
    masked = jnp.concatenate([jnp.where(node == node_row, plane, 0.0) for plane in planes], axis=0)
    pick_row = lax.broadcasted_iota(jnp.int32, (rows, 128), 0)
    pick_lane = lax.broadcasted_iota(jnp.int32, (rows, 128), 1)
    pick = jnp.where(lax.rem(pick_row, length_z) == pick_lane, 1.0, 0.0).astype(BF16)
    masked_hi, masked_lo = split(masked)
    flat = jnp.dot(masked_hi, pick, preferred_element_type=F32) + jnp.dot(
        masked_lo, pick, preferred_element_type=F32
    )
    bundle = flat[0:8]
    tiles = 4 * length_x // 8
    for tile in range(1, tiles):
        bundle = bundle + pltpu.roll(flat[tile * 8 : tile * 8 + 8], tile * length_z, 1)
    pull_send[...] = bundle
    reach = 2 * REACH + 1
    folded = n_span == 2 * REACH
    pull_copies = []
    offsets = [
        (dx, dz)
        for dx in range(-REACH, REACH + 1)
        for dz in range(-REACH, REACH + 1)
        if (dx, dz) != (0, 0) and not (folded and dz == REACH)
    ]
    for dx, dz in sorted(offsets, key=lambda pair: -abs(pair[0]) - abs(pair[1])):
        slot = (REACH - dx) * reach + (REACH - dz)
        copy = remote(
            pull_send, pull_got.at[slot], pull_ss.at[slot], pull_rs.at[slot], at(dx, dz)
        )
        copy.start()
        pull_copies.append(copy)

    add_faces(0, copies_one)
    operate(1, 1)
    copies_two = send_faces(1)
    for c in range(3):
        field[2, c] = local[1, c]
    lines_rows = jnp.concatenate([lines_mass, lines[1] / height], axis=1)
    ends = [lines_rows[0:1], lines_rows[length_y - 1 : length_y]]
    once = [(end[:, :length_y], end[:, length_y:]) for end in ends]
    twice = dot3(
        split(jnp.concatenate([once[0][0], once[0][1], once[1][0], once[1][1]] * 2, axis=0)),
        (lines_hi, lines_lo),
        NN,
    )
    one_lane = lax.broadcasted_iota(jnp.int32, (1, length_y), 1)
    zero = jnp.zeros((1, length_y), F32)
    images = []
    for side in range(2):
        tip = jnp.where(one_lane == side * (length_y - 1), 1.0, 0.0)
        by_mass, by_stiff = twice[2 * side : 2 * side + 1], twice[2 * side + 1 : 2 * side + 2]
        rows_of = [
            (tip, zero, zero),
            (zero, once[side][0], zero),
            (zero, once[side][1], zero),
            (zero, zero, by_mass[:, :length_y]),
            (zero, zero, by_stiff[:, :length_y]),
            (zero, zero, by_mass[:, length_y:]),
            (zero, zero, by_stiff[:, length_y:]),
        ]
        for entry in rows_of:
            image = jnp.concatenate(entry, axis=1)
            images.append(jnp.broadcast_to(image, (length_z, 3 * length_y)))
        images.append(jnp.zeros((128 - 7 * length_z, 3 * length_y), F32))
    images = split(jnp.concatenate(images, axis=0))
    words_x_parts = split(words_x[...])
    words_z_parts = split(words_z[...])

    for copy in pull_copies:
        copy.wait()
    small_lane = lax.broadcasted_iota(jnp.int32, (8, 128), 1) // length_z
    spans = []
    for ix in range(reach):
        pieces = [
            bundle
            if (ix, iz) == (REACH, REACH)
            else pull_got[ix * reach + (reach - 1 if folded and iz == 0 else iz)]
            for iz in range(reach)
        ]
        for tile in range(tiles):
            line = jnp.zeros((8, 128), F32)
            for iz in range(reach):
                shift = ((iz - tile) * length_z) % 128
                moved = pltpu.roll(pieces[iz], shift, 1) if shift else pieces[iz]
                line = jnp.where(small_lane == iz, moved, line)
            spans.append(line)
    along_z = dot3(split(jnp.concatenate(spans, axis=0)), words_z_parts, NT)
    by_plane = []
    for plane in range(4):
        by_plane.append(
            jnp.concatenate(
                [
                    along_z[(ix * 4 + plane) * length_x : (ix * 4 + plane + 1) * length_x]
                    for ix in range(reach)
                ],
                axis=0,
            )
        )
    both_ways = dot3(words_x_parts, split(jnp.concatenate(by_plane, axis=1)), NN)
    block_lane = lax.broadcasted_iota(jnp.int32, (length_x, 128), 1) // length_z
    keep_row = lax.rem(lax.broadcasted_iota(jnp.int32, (rows, 256), 0), length_z)
    keep_lane = lax.rem(lax.broadcasted_iota(jnp.int32, (rows, 256), 1), length_z)
    tractions = []
    for index in range(2):
        blocks = []
        for side in range(2):
            plane = index * 2 + side
            total = jnp.zeros((length_x, 128), F32)
            for block, word_x, word_z in TERMS:
                piece = both_ways[
                    word_x * length_x : (word_x + 1) * length_x, plane * 128 : plane * 128 + 128
                ]
                shift = ((block - word_z) * length_z) % 128
                moved = pltpu.roll(piece, shift, 1) if shift else piece
                total = total + jnp.where(block_lane == block, moved, 0.0)
            blocks.append(total)
        wide = jnp.concatenate(blocks, axis=1)
        tall = jnp.concatenate(
            [jnp.broadcast_to(wide[x : x + 1], (length_z, 256)) for x in range(length_x)], axis=0
        )
        tall = jnp.where(keep_row == keep_lane, tall, 0.0)
        tractions.append(dot3(split(tall), images, NN))
    add_faces(1, copies_two)
    t1, t2 = shifts
    for c in range(3):
        chain = [field[level, c] for level in range(3)]
        if c != 1:
            taus = tractions[c // 2]
            chain = [
                chain[level] + taus[:, level * length_y : (level + 1) * length_y]
                for level in range(3)
            ]
        v1 = chain[1] - t1 * chain[0]
        field[0, c] = chain[0]
        field[1, c] = v1
        field[2, c] = chain[2] - t1 * chain[1] - t2 * v1
    operate(2, 2)
    for newest in range(3):
        inner_products(newest)
    for c in range(3):
        inner(6, c, field[2, c] * columns[2] * local[2, c])

    total_rows = parts.shape[0]
    r_iota = lax.broadcasted_iota(jnp.int32, (total_rows, 128), 0)
    l_iota = lax.broadcasted_iota(jnp.int32, (total_rows, 128), 1)
    diagonal = r_iota == l_iota
    summed = jnp.sum(parts[...], axis=1, keepdims=True)
    row = jnp.sum(jnp.where(diagonal, summed, 0.0), axis=0, keepdims=True)

    def gather_sum(stage, row, count, got, ss, rs, place):
        sum_send[stage : stage + 1, :] = row
        copies = []
        for k in range(1, count):
            copy = remote(
                sum_send.at[pl.ds(stage, 1), :],
                got.at[pl.ds(k - 1, 1), :],
                ss.at[k - 1],
                rs.at[k - 1],
                place(k),
            )
            copy.start()
            copies.append(copy)
        for copy in copies:
            copy.wait()
        return row + jnp.sum(got[...], axis=0, keepdims=True)

    if single:
        every = n_wall * n_span
        row = gather_sum(
            0, row, every, wall_got, wall_ss, wall_rs, lambda k: at(k // n_span, k % n_span)
        )
    else:
        row = gather_sum(0, row, n_wall, wall_got, wall_ss, wall_rs, lambda k: at(k, 0))
        row = gather_sum(1, row, n_span, span_got, span_ss, span_rs, lambda k: at(0, k))
    totals = jnp.sum(jnp.where(diagonal, row, 0.0), axis=1, keepdims=True)
    m00, m01, m11, m02, m12, m22, e22 = [totals[q * 8 : q * 8 + 8, :] for q in range(7)]
    t1, t2 = shifts
    a00 = m01 + t1 * m00
    a01 = m11 + t1 * m01
    a02 = m12 + t1 * m02
    a11 = m12 + t2 * m11
    a12 = m22 + t2 * m12
    l10 = a01 / a00
    l20 = a02 / a00
    d1 = a11 - l10 * a01
    u12 = a12 - l10 * a02
    l21 = u12 / d1
    d2 = e22 - l20 * a02 - l21 * u12
    y1 = m01 - l10 * m00
    y2 = m02 - l20 * m00 - l21 * y1
    x2 = y2 / d2
    x1 = y1 / d1 - l21 * x2
    x0 = m00 / a00 - l10 * x1 - l20 * x2
    for c in range(3):
        result = (
            x0[c : c + 1] * field[0, c] + x1[c : c + 1] * field[1, c] + x2[c : c + 1] * field[2, c]
        )
        out[c] = result.reshape(length_x, length_z, length_y)


def body(n_wall, n_span, velocity_old, heights, owner_device, owner_element, ref_coords, roughness):
    sizes = velocity_old.shape[1:]
    length_x, length_z, length_y = sizes
    rows = length_x * length_z
    points = owner_device.shape[0]
    both, lines, columns, words_x, words_z = tables(*sizes)
    plane_hi, plane_lo = split_np(both)
    every = n_wall * n_span
    first = every if every <= SINGLE_STAGE else n_wall
    vmem = pl.BlockSpec(memory_space=pltpu.VMEM)
    hbm = pl.BlockSpec(memory_space=pltpu.HBM)
    operands = (
        velocity_old,
        heights.reshape(1, -1),
        owner_device.reshape(1, -1),
        owner_element.reshape(1, -1),
        ref_coords,
        roughness.reshape(1, -1),
        plane_hi,
        plane_lo,
        jnp.asarray(lines, F32),
        jnp.asarray(columns, F32),
        jnp.asarray(words_x, F32),
        jnp.asarray(words_z, F32),
    )
    dma = pltpu.SemaphoreType.DMA
    return pl.pallas_call(
        functools.partial(kernel, n_wall, n_span, sizes),
        out_shape=(
            jax.ShapeDtypeStruct(velocity_old.shape, F32),
            jax.ShapeDtypeStruct((2, points), F32),
        ),
        in_specs=[hbm] * 12,
        out_specs=(vmem, vmem),
        scratch_shapes=[pltpu.VMEM(value.shape, value.dtype) for value in operands]
        + [
            dma((12,)),
            pltpu.VMEM((2, 64, length_y), F32),
            pltpu.VMEM((2, 2, 64, length_y), F32),
            pltpu.VMEM((3, 3, rows, length_y), F32),
            pltpu.VMEM((3, 3, rows, length_y), F32),
            pltpu.VMEM((ROUNDS, 2, 3, length_x, length_y), F32),
            pltpu.VMEM((ROUNDS, 4, 8, length_y), F32),
            pltpu.VMEM((ROUNDS, 2, 3, length_z, length_y), F32),
            pltpu.VMEM((ROUNDS, 2, 3, length_x, length_y), F32),
            pltpu.VMEM((ROUNDS, 4, 8, length_y), F32),
            pltpu.VMEM((56, length_y), F32),
            pltpu.VMEM((2, 128), F32),
            pltpu.VMEM((first - 1, 128), F32),
            pltpu.VMEM((n_span - 1, 128), F32),
            pltpu.VMEM((8, 128), F32),
            pltpu.VMEM((25, 8, 128), F32),
            dma((25,)),
            dma((25,)),
            dma((2,)),
            dma((2,)),
            dma((ROUNDS, 8)),
            dma((ROUNDS, 8)),
            dma((first - 1,)),
            dma((first - 1,)),
            dma((n_span - 1,)),
            dma((n_span - 1,)),
        ],
        compiler_params=pltpu.CompilerParams(
            collective_id=0, has_side_effects=True, vmem_limit_bytes=67043328
        ),
    )(*operands)


def solution(mesh):
    placed = (
        P(None, "wall", "span", None),
        P(),
        P(("wall", "span"), None),
        P(("wall", "span"), None),
        P(None, ("wall", "span")),
        P(("wall", "span")),
    )
    return jax.shard_map(
        functools.partial(body, mesh.shape["wall"], mesh.shape["span"]),
        mesh=mesh,
        in_specs=placed,
        out_specs=(P(None, "wall", "span", None), P(None, ("wall", "span"))),
        check_vma=False,
    )
```

profile of v0, /device:TPU:0, one launch (start us, length us, event | category | flops | bytes accessed | tf_op | source)
XLA Modules:
  0.0 29.0 jit_solution(13631217772030951240)
XLA Ops:
  0.6 26.0 %shard_map.131 = (f32[3,16,16,128]{3,2,1,0:T(8,128)}, f32[2,512]{1,0:T(2,128)}) custom-call(f32[3,16,16,128]{3,2,1,0:T(8,128)} %vel_in.1, f32[1,16]{1,0:T(1,128)} %bitcast.7, s32[1,512]{1,0:T(1,128)} %bitcast.4, s32[1,512]{1,0:T(1,128)} %bitcast.5, f32[3,512]{1,0:T(4,128)} %coords_in.1, f32[1,512]{1,0:T(1,128)} %bitcast.6, ...), custom_call_target="tpu_custom_call" | custom-call | tf_op jit(solution)/shard_map/pallas_call | solution.py:731
  26.6 0.0 copy-start
  26.6 1.8 %copy.16 = f32[3,16,16,128]{3,2,1,0:T(8,128)} copy(f32[3,16,16,128]{3,2,1,0:T(8,128)} %get-tuple-element.4) | data formatting | bytes 786432
  28.4 0.0 copy-done
  28.4 0.6 %copy.17 = f32[2,512]{1,0:T(2,128)} copy(f32[2,512]{1,0:T(2,128)S(1)} %copy-done) | data formatting | bytes 8192
Async XLA Ops:
  26.6 1.8 %copy-start = (f32[2,512]{1,0:T(2,128)S(1)}, f32[2,512]{1,0:T(2,128)}, u32[]{:S(2)}) copy-start(f32[2,512]{1,0:T(2,128)} %get-tuple-element.5) | copy-start | bytes 12292
where the time goes:
time: 29.2 us; the launch traced here: 29 us
  Pallas kernels  26 us (89%)
  local copies, waits for them, and re-layouts  2.36 us (8%)
  between operations  0.65 us (2%)
    pallas_call x1, Pallas kernels, body(): pl.pallas_call(functools.partial(kernel, n_wall, n_span, sizes), out_shap...  26 us
    unnamed x4, local copies, waits for them, and re-layouts  2.36 us

commit v1 on v0

--- a/solution.py
+++ b/solution.py
@@ -54,6 +54,7 @@
     (6, 6, 6),
 )
 SINGLE_STAGE = 64
+VMEM_LIMIT = 32 * 2**20
 MESH = pl.DeviceIdType.MESH
 F32 = jnp.float32
 BF16 = jnp.bfloat16
@@ -220,7 +221,8 @@
     columns_in,
     words_x_in,
     words_z_in,
-    out,
+    field,
+    factors,
     neumann,
     vel,
     heights,
@@ -237,13 +239,9 @@
     load_sem,
     near,
     near_got,
-    field,
     local,
-    z_send,
-    c_send,
-    x_got,
-    z_got,
-    c_got,
+    face_send,
+    face_got,
     parts,
     sum_send,
     wall_got,
@@ -348,74 +346,52 @@
             device_id_type=MESH,
         )
 
-    def face_copies(turn):
-        copies = []
-        for slot, dx in enumerate((1, -1)):
-            start = rows - length_z if dx == 1 else 0
-            copies.append(
-                remote(
-                    local.at[turn, :, pl.ds(start, length_z), :],
-                    x_got.at[turn, slot],
-                    face_ss.at[turn, slot],
-                    face_rs.at[turn, slot],
-                    at(dx, 0),
-                )
-            )
-        for slot, dz in enumerate((1, -1)):
-            copies.append(
-                remote(
-                    z_send.at[turn, slot],
-                    z_got.at[turn, slot],
-                    face_ss.at[turn, 2 + slot],
-                    face_rs.at[turn, 2 + slot],
-                    at(0, dz),
-                )
-            )
-        for slot, (dx, dz) in enumerate(DIRS):
-            copies.append(
-                remote(
-                    c_send.at[turn, slot, pl.ds(0, 3), :],
-                    c_got.at[turn, slot, pl.ds(0, 3), :],
-                    face_ss.at[turn, 4 + slot],
-                    face_rs.at[turn, 4 + slot],
-                    at(dx, dz),
-                )
-            )
-        return copies
+    face_rows = []
+    for slot, (dx, dz) in enumerate(((1, 0), (-1, 0), (0, 1), (0, -1)) + DIRS):
+        size = 3 * (1 if dx and dz else length_z if dx else length_x)
+        face_rows.append((sum(entry[1] for entry in face_rows), size, dx, dz))
+    face_total = sum(entry[1] for entry in face_rows)
 
     def corner(dx, dz):
         return (rows - length_z if dx == 1 else 0) + (length_z - 1 if dz == 1 else 0)
 
+    def face_part(slot, c, dx, dz):
+        first, size = face_rows[slot][0] + c * (face_rows[slot][1] // 3), face_rows[slot][1] // 3
+        if dx and dz:
+            rows_of = pl.ds(corner(dx, dz), 1)
+        elif dx:
+            rows_of = pl.ds(rows - length_z if dx == 1 else 0, length_z)
+        else:
+            rows_of = pl.ds(length_z - 1 if dz == 1 else 0, length_x, stride=length_z)
+        return pl.ds(first, size), rows_of
+
     def send_faces(turn):
         for c in range(3):
-            for slot, dz in enumerate((1, -1)):
-                edge = length_z - 1 if dz == 1 else 0
-                z_send[turn, slot, c] = local[turn, c, pl.ds(edge, length_x, stride=length_z), :]
-            for slot, (dx, dz) in enumerate(DIRS):
-                at_row = corner(dx, dz)
-                c_send[turn, slot, c : c + 1, :] = local[turn, c, at_row : at_row + 1, :]
+            for slot, (_, _, dx, dz) in enumerate(face_rows):
+                packed_rows, rows_of = face_part(slot, c, dx, dz)
+                face_send[turn, packed_rows, :] = local[turn, c, rows_of, :]
         if turn == 0:
             pl.semaphore_wait(barrier, len(greeted))
             for copy in near_copies:
                 copy.start()
-        copies = face_copies(turn)
-        for copy in copies:
-            copy.start()
-        return copies
-
-    def add_faces(turn, copies):
-        for copy in copies:
-            copy.wait()
+        for first, size, dx, dz in face_rows:
+            part = (turn, pl.ds(first, size), slice(None))
+            remote(
+                face_send.at[part], face_got.at[part], face_ss.at[turn], face_rs.at[turn], at(dx, dz)
+            ).start()
+
+    def settle(ss, rs, ref):
+        for semaphore in (rs, ss):
+            pltpu.make_async_copy(ref, ref, semaphore).wait()
+
+    def add_faces(turn):
+        settle(face_ss.at[turn], face_rs.at[turn], face_got.at[turn, pl.ds(0, face_total), :])
         for c in range(3):
-            for slot, dx in enumerate((1, -1)):
-                start = 0 if dx == 1 else rows - length_z
-                field[turn + 1, c, pl.ds(start, length_z), :] += x_got[turn, slot, c]
-            for slot, dz in enumerate((1, -1)):
-                edge = pl.ds(0 if dz == 1 else length_z - 1, length_x, stride=length_z)
-                field[turn + 1, c, edge, :] = field[turn + 1, c, edge, :] + z_got[turn, slot, c]
-            for slot, (dx, dz) in enumerate(DIRS):
-                at_row = corner(-dx, -dz)
-                field[turn + 1, c, at_row : at_row + 1, :] += c_got[turn, slot, c : c + 1, :]
+            for slot, (_, _, dx, dz) in enumerate(face_rows):
+                packed_rows, rows_of = face_part(slot, c, -dx, -dz)
+                field[turn + 1, c, rows_of, :] = (
+                    field[turn + 1, c, rows_of, :] + face_got[turn, packed_rows, :]
+                )
 
     def inner(quantity, c, product):
         parts[quantity * 8 + c : quantity * 8 + c + 1, :] = jnp.sum(
@@ -452,11 +428,11 @@
 
     near_copies = []
     for slot, dx in enumerate((1, -1)):
-        copy = remote(near, near_got.at[slot], near_ss.at[slot], near_rs.at[slot], at(dx, 0))
+        copy = remote(near, near_got.at[slot], near_ss, near_rs, at(dx, 0))
         near_copies.append(copy)
 
     operate(0, 0)
-    copies_one = send_faces(0)
+    send_faces(0)
     for c in range(3):
         field[1, c] = local[0, c]
     parts[...] = jnp.zeros_like(parts)
@@ -480,8 +456,7 @@
     along = jnp.where(wanted, jnp.concatenate([row_y] * (length_y // 8), axis=0), 0.0)
     spread = split(spread)
 
-    for copy in near_copies:
-        copy.wait()
+    settle(near_ss, near_rs, near_got)
 
     sampled = []
     for index in range(2):
@@ -519,7 +494,6 @@
     pull_send[...] = bundle
     reach = 2 * REACH + 1
     folded = n_span == 2 * REACH
-    pull_copies = []
     offsets = [
         (dx, dz)
         for dx in range(-REACH, REACH + 1)
@@ -528,15 +502,11 @@
     ]
     for dx, dz in sorted(offsets, key=lambda pair: -abs(pair[0]) - abs(pair[1])):
         slot = (REACH - dx) * reach + (REACH - dz)
-        copy = remote(
-            pull_send, pull_got.at[slot], pull_ss.at[slot], pull_rs.at[slot], at(dx, dz)
-        )
-        copy.start()
-        pull_copies.append(copy)
-
-    add_faces(0, copies_one)
+        remote(pull_send, pull_got.at[slot], pull_ss, pull_rs, at(dx, dz)).start()
+
+    add_faces(0)
     operate(1, 1)
-    copies_two = send_faces(1)
+    send_faces(1)
     for c in range(3):
         field[2, c] = local[1, c]
     lines_rows = jnp.concatenate([lines_mass, lines[1] / height], axis=1)
@@ -570,8 +540,7 @@
     words_x_parts = split(words_x[...])
     words_z_parts = split(words_z[...])
 
-    for copy in pull_copies:
-        copy.wait()
+    settle(pull_ss, pull_rs, pull_got.at[pl.ds(0, len(offsets))])
     small_lane = lax.broadcasted_iota(jnp.int32, (8, 128), 1) // length_z
     spans = []
     for ix in range(reach):
@@ -624,7 +593,7 @@
         )
         tall = jnp.where(keep_row == keep_lane, tall, 0.0)
         tractions.append(dot3(split(tall), images, NN))
-    add_faces(1, copies_two)
+    add_faces(1)
     t1, t2 = shifts
     for c in range(3):
         chain = [field[level, c] for level in range(3)]
@@ -653,19 +622,11 @@
 
     def gather_sum(stage, row, count, got, ss, rs, place):
         sum_send[stage : stage + 1, :] = row
-        copies = []
         for k in range(1, count):
-            copy = remote(
-                sum_send.at[pl.ds(stage, 1), :],
-                got.at[pl.ds(k - 1, 1), :],
-                ss.at[k - 1],
-                rs.at[k - 1],
-                place(k),
-            )
-            copy.start()
-            copies.append(copy)
-        for copy in copies:
-            copy.wait()
+            remote(
+                sum_send.at[pl.ds(stage, 1), :], got.at[pl.ds(k - 1, 1), :], ss, rs, place(k)
+            ).start()
+        settle(ss, rs, got)
         return row + jnp.sum(got[...], axis=0, keepdims=True)
 
     if single:
@@ -695,11 +656,25 @@
     x2 = y2 / d2
     x1 = y1 / d1 - l21 * x2
     x0 = m00 / a00 - l10 * x1 - l20 * x2
+    for index, value in enumerate((x0, x1, x2)):
+        factors[index] = jnp.broadcast_to(value, (8, 128))
+
+
+def combine(field, factors, neumann_in, out, neumann, stage, sems):
+    small = pltpu.make_async_copy(neumann_in, neumann, sems.at[3])
+    small.start()
+    copies = []
     for c in range(3):
-        result = (
-            x0[c : c + 1] * field[0, c] + x1[c : c + 1] * field[1, c] + x2[c : c + 1] * field[2, c]
-        )
-        out[c] = result.reshape(length_x, length_z, length_y)
+        result = factors[0, c : c + 1] * field[0, c]
+        for level in range(1, 3):
+            result += factors[level, c : c + 1] * field[level, c]
+        stage[c] = result.reshape(stage.shape[1:])
+        copy = pltpu.make_async_copy(stage.at[c], out.at[c], sems.at[c])
+        copy.start()
+        copies.append(copy)
+    for copy in copies:
+        copy.wait()
+    small.wait()
 
 
 def body(n_wall, n_span, velocity_old, heights, owner_device, owner_element, ref_coords, roughness):
@@ -711,6 +686,7 @@
     plane_hi, plane_lo = split_np(both)
     every = n_wall * n_span
     first = every if every <= SINGLE_STAGE else n_wall
+    faces = -(-(6 * (length_x + length_z) + 12) // 8) * 8
     vmem = pl.BlockSpec(memory_space=pltpu.VMEM)
     hbm = pl.BlockSpec(memory_space=pltpu.HBM)
     operands = (
@@ -728,47 +704,55 @@
         jnp.asarray(words_z, F32),
     )
     dma = pltpu.SemaphoreType.DMA
-    return pl.pallas_call(
+    field, factors, neumann = pl.pallas_call(
         functools.partial(kernel, n_wall, n_span, sizes),
         out_shape=(
-            jax.ShapeDtypeStruct(velocity_old.shape, F32),
-            jax.ShapeDtypeStruct((2, points), F32),
+            pltpu.VMEM((3, 3, rows, length_y), F32),
+            pltpu.VMEM((3, 8, 128), F32),
+            pltpu.VMEM((2, points), F32),
         ),
         in_specs=[hbm] * 12,
-        out_specs=(vmem, vmem),
+        out_specs=(vmem, vmem, vmem),
         scratch_shapes=[pltpu.VMEM(value.shape, value.dtype) for value in operands]
         + [
             dma((12,)),
             pltpu.VMEM((2, 64, length_y), F32),
             pltpu.VMEM((2, 2, 64, length_y), F32),
             pltpu.VMEM((3, 3, rows, length_y), F32),
-            pltpu.VMEM((3, 3, rows, length_y), F32),
-            pltpu.VMEM((ROUNDS, 2, 3, length_x, length_y), F32),
-            pltpu.VMEM((ROUNDS, 4, 8, length_y), F32),
-            pltpu.VMEM((ROUNDS, 2, 3, length_z, length_y), F32),
-            pltpu.VMEM((ROUNDS, 2, 3, length_x, length_y), F32),
-            pltpu.VMEM((ROUNDS, 4, 8, length_y), F32),
+            pltpu.VMEM((ROUNDS, faces, length_y), F32),
+            pltpu.VMEM((ROUNDS, faces, length_y), F32),
             pltpu.VMEM((56, length_y), F32),
             pltpu.VMEM((2, 128), F32),
             pltpu.VMEM((first - 1, 128), F32),
             pltpu.VMEM((n_span - 1, 128), F32),
             pltpu.VMEM((8, 128), F32),
             pltpu.VMEM((25, 8, 128), F32),
-            dma((25,)),
-            dma((25,)),
-            dma((2,)),
-            dma((2,)),
-            dma((ROUNDS, 8)),
-            dma((ROUNDS, 8)),
-            dma((first - 1,)),
-            dma((first - 1,)),
-            dma((n_span - 1,)),
-            dma((n_span - 1,)),
+            dma,
+            dma,
+            dma,
+            dma,
+            dma((ROUNDS,)),
+            dma((ROUNDS,)),
+            dma,
+            dma,
+            dma,
+            dma,
         ],
         compiler_params=pltpu.CompilerParams(
-            collective_id=0, has_side_effects=True, vmem_limit_bytes=67043328
+            collective_id=0, has_side_effects=True, vmem_limit_bytes=VMEM_LIMIT
         ),
-    )(*operands)
+    )(*[pltpu.with_memory_space_constraint(value, pltpu.HBM) for value in operands])
+    return pl.pallas_call(
+        combine,
+        out_shape=(
+            jax.ShapeDtypeStruct(velocity_old.shape, F32),
+            jax.ShapeDtypeStruct((2, points), F32),
+        ),
+        in_specs=[vmem] * 3,
+        out_specs=(hbm, hbm),
+        scratch_shapes=[pltpu.VMEM(velocity_old.shape, F32), dma((4,))],
+        compiler_params=pltpu.CompilerParams(vmem_limit_bytes=VMEM_LIMIT),
+    )(field, factors, neumann)
 
 
 def solution(mesh):

time: 29.2 us -> 25.4 us (0.87)
  local copies, waits for them, and re-layouts: 2.36 us -> 0 us
  Pallas kernels: 26 us -> 24.6 us
    unnamed x4 -> x0, local copies, waits for them, and re-layouts: 2.36 us -> none
    pallas_call x1, Pallas kernels: 26 us -> 23.8 us  [body(): pl.pallas_call(functools.partial(kernel, n_wall, n_span, sizes), out_shap...]
    pallas_call x0 -> x1, Pallas kernels: none -> 0.8 us  [body(): pl.pallas_call(combine, out_shape=(jax.ShapeDtypeStruct(velocity_old.shap...]
where the time goes in v1:
time: 25.4 us; the launch traced here: 25.3 us
  Pallas kernels  24.6 us (97%)
  between operations  0.64 us (3%)
    pallas_call x1, Pallas kernels, body(): pl.pallas_call(functools.partial(kernel, n_wall, n_span, sizes), out_shap...  23.8 us
    pallas_call x1, Pallas kernels, body(): pl.pallas_call(combine, out_shape=(jax.ShapeDtypeStruct(velocity_old.shap...  0.8 us

profile of v1, /device:TPU:0, one launch (start us, length us, event | category | flops | bytes accessed | tf_op | source)
XLA Modules:
  0.0 25.3 jit_solution(9544857298772001520)
XLA Ops:
  0.6 23.8 %shard_map.131 = (f32[3,3,256,128]{3,2,1,0:T(8,128)S(1)}, f32[3,8,128]{2,1,0:T(8,128)S(1)}, f32[2,512]{1,0:T(2,128)S(1)}) custom-call(f32[3,16,16,128]{3,2,1,0:T(8,128)} %vel_in.1, f32[1,16]{1,0:T(1,128)} %bitcast.7, s32[1,512]{1,0:T(1,128)} %bitcast.4, s32[1,512]{1,0:T(1,128)} %bitcast.5, f32[3,512]{1,0:T(4,128)} %coords_in.1, f32[1,512]{1,0:T(1,128)} %bitcast.6, ...), custom_call_target="tpu_custom_call" | custom-call | tf_op jit(solution)/shard_map/pallas_call | solution.py:707
  24.5 0.8 %shard_map.132 = (f32[3,16,16,128]{3,2,1,0:T(8,128)}, f32[2,512]{1,0:T(2,128)}) custom-call(f32[3,3,256,128]{3,2,1,0:T(8,128)S(1)} %get-tuple-element.5.field, f32[3,8,128]{2,1,0:T(8,128)S(1)} %get-tuple-element.6.factors, f32[2,512]{1,0:T(2,128)S(1)} %get-tuple-element.7.neumann_in), custom_call_target="tpu_custom_call" | custom-call | tf_op jit(solution)/shard_map/pallas_call | solution.py:745

commit v2 on v1

--- a/solution.py
+++ b/solution.py
@@ -122,8 +122,7 @@
         np.kron(stiff_x, np.diag(mass_z)) + np.kron(np.diag(mass_x), stiff_z)
     ) + inverse_step * np.diag(mass_xz)
     plane = join_xz @ plane
-    mass_plane = join_xz @ np.diag(mass_xz)
-    both = np.concatenate([plane, mass_plane], axis=1)
+    mass_plane = join_xz @ mass_xz
     lines_mass = np.tile(0.5 * weights, count_y)[:, None] * join_y
     lines_stiff = viscosity * 2.0 * (np.kron(np.eye(count_y), stiffness) @ join_y)
     lines = np.stack([lines_mass, lines_stiff])
@@ -138,14 +137,10 @@
     inner_z = face_weights(length_z, True)
     outer_x = face_weights(length_x, False)
     outer_z = face_weights(length_z, False)
-    weight_y = face_weights(length_y, True)
     columns = np.stack(
-        [
-            assembled[:, None] * np.ones(length_y)[None],
-            np.kron(outer_x, outer_z)[:, None] * weight_y[None],
-            np.kron(inner_x, inner_z)[:, None] * weight_y[None],
-        ]
+        [assembled, mass_plane, np.kron(outer_x, outer_z), np.kron(inner_x, inner_z)]
     )
+    columns = columns[:, :, None] * np.ones(length_y)[None, None]
     reach = 2 * REACH + 1
 
     def words(length, mass, stiff, extra):
@@ -170,7 +165,9 @@
     words_z = words(length_z, mass_z, stiffness * (2.0 / element_dz), inverse_step)
     pad = np.zeros((128, 128 - reach * length_z))
     words_z = np.concatenate([words_z, pad], axis=1)
-    return both, lines, columns, words_x, words_z
+    pad = np.zeros((128, 128 - reach * length_x))
+    words_x = np.concatenate([words_x, pad], axis=1)
+    return plane, lines, columns, words_x, words_z
 
 
 def split(value):
@@ -215,12 +212,10 @@
     element_in,
     coords_in,
     roughness_in,
-    plane_hi_in,
-    plane_lo_in,
+    plane_in,
     lines_in,
     columns_in,
-    words_x_in,
-    words_z_in,
+    words_in,
     field,
     factors,
     neumann,
@@ -230,12 +225,10 @@
     element,
     coords,
     roughness,
-    plane_hi,
-    plane_lo,
+    sheet,
     lines,
     columns,
-    words_x,
-    words_z,
+    words,
     load_sem,
     near,
     near_got,
@@ -268,27 +261,30 @@
     def at(dx, dz):
         return (lax.rem(w + (dx + n_wall), n_wall), lax.rem(s + (dz + n_span), n_span))
 
-    loads = [
-        pltpu.make_async_copy(source, target, load_sem.at[index])
-        for index, (source, target) in enumerate(
+    loads = {
+        name: pltpu.make_async_copy(source, target, load_sem.at[index])
+        for index, (name, source, target) in enumerate(
             (
-                (vel_in, vel),
-                (heights_in, heights),
-                (lines_in, lines),
-                (coords_in, coords),
-                (owner_in, owner),
-                (element_in, element),
-                (columns_in, columns),
-                (roughness_in, roughness),
-                (plane_hi_in, plane_hi),
-                (plane_lo_in, plane_lo),
-                (words_x_in, words_x),
-                (words_z_in, words_z),
+                ("vel", vel_in, vel),
+                ("heights", heights_in, heights),
+                ("lines", lines_in, lines),
+                ("scale", columns_in.at[pl.ds(0, 2)], columns.at[pl.ds(0, 2)]),
+                ("plane", plane_in, sheet),
+                ("coords", coords_in, coords),
+                ("owner", owner_in, owner),
+                ("element", element_in, element),
+                ("roughness", roughness_in, roughness),
+                ("words", words_in, words),
+                ("weights", columns_in.at[pl.ds(2, 2)], columns.at[pl.ds(2, 2)]),
             )
         )
-    ]
-    for load in loads:
+    }
+    for load in loads.values():
         load.start()
+
+    def loaded(*names):
+        for name in names:
+            loads[name].wait()
 
     single = n_wall * n_span <= SINGLE_STAGE
     if single:
@@ -308,7 +304,7 @@
     for dx, dz in greeted:
         pl.semaphore_signal(barrier, inc=1, device_id=at(dx, dz), device_id_type=MESH)
 
-    loads[0].wait()
+    loaded("vel")
     lane = lax.broadcasted_iota(jnp.int32, (64, length_y), 1)
     groups = (length_x // 8) * count_z
     for index, comp in enumerate((0, 2)):
@@ -319,15 +315,22 @@
             moved = pltpu.roll(block, (group * 32 + 16) % length_y, 1)
             packed = jnp.where(lane // 32 == group, moved, packed)
         near[index] = packed
-    for load in loads[1:]:
-        load.wait()
+    loaded("heights", "lines", "scale", "plane")
 
     layer_of = lax.broadcasted_iota(jnp.int32, (length_y, count_y), 0) // 8
     layer = lax.broadcasted_iota(jnp.int32, (length_y, count_y), 1)
     height_row = heights[...]
     height = jnp.sum(jnp.where(layer_of == layer, height_row, 0.0), axis=1, keepdims=True)
     lines_mass = height * lines[0]
-    lines_hi, lines_lo = split(jnp.concatenate([lines_mass, lines[1] / height], axis=1))
+    lines_stiff = lines[1] / height
+    stiff_hi, stiff_lo = split(lines_stiff)
+    lines_packed = jnp.concatenate(
+        [
+            jnp.concatenate([stiff_hi, stiff_lo], axis=1),
+            jnp.concatenate([stiff_hi, jnp.zeros_like(stiff_lo)], axis=1),
+        ],
+        axis=0,
+    )
     bound = jnp.max(0.1535 * height_row + 0.000182 / height_row, axis=1, keepdims=True)
     shifts = (0.15 * bound, 0.85 * bound)
 
@@ -399,30 +402,31 @@
         )
 
     def operate(source, target):
-        flat = field[source].reshape(3 * rows, length_y)
-        lined = dot3(split(flat), (lines_hi, lines_lo), NN)
-        wide = jnp.concatenate(
-            [
-                jnp.concatenate(
-                    [
-                        lined[c * rows : (c + 1) * rows, :length_y],
-                        lined[c * rows : (c + 1) * rows, length_y:],
-                    ],
-                    axis=0,
-                )
-                for c in range(3)
-            ],
-            axis=1,
-        )
-        result = dot3((plane_hi[...], plane_lo[...]), split(wide), NN)
+        highs, lows = zip(*[split(field[source, c]) for c in range(3)])
+        along_y = jnp.dot(
+            jnp.concatenate(
+                [jnp.concatenate([high, low], axis=1) for high, low in zip(highs, lows)], axis=0
+            ),
+            lines_packed,
+            preferred_element_type=F32,
+        )
+        across = jnp.dot(
+            sheet[0], jnp.concatenate(highs + lows, axis=1), preferred_element_type=F32
+        )
+        across_low = jnp.dot(sheet[1], jnp.concatenate(highs, axis=1), preferred_element_type=F32)
         for c in range(3):
-            local[target, c] = result[:, c * length_y : (c + 1) * length_y]
+            here = slice(c * length_y, (c + 1) * length_y)
+            also = slice((3 + c) * length_y, (4 + c) * length_y)
+            flat = across[:, here] + (across[:, also] + across_low[:, here])
+            tall = along_y[c * rows : (c + 1) * rows]
+            tall = tall[:, :length_y] + tall[:, length_y:]
+            local[target, c] = flat * mass_row + tall * columns[1]
 
     slots = {(0, 0): 0, (0, 1): 1, (1, 1): 2, (0, 2): 3, (1, 2): 4, (2, 2): 5}
 
     def inner_products(newest):
         for c in range(3):
-            weighted = field[newest, c] * columns[1]
+            weighted = field[newest, c] * columns[2]
             for other in range(newest + 1):
                 inner(slots[(other, newest)], c, weighted * field[other, c])
 
@@ -437,6 +441,7 @@
         field[1, c] = local[0, c]
     parts[...] = jnp.zeros_like(parts)
 
+    loaded("coords", "owner", "element", "roughness")
     points = owner.shape[1]
     row_x = lagrange_rows(coords[0:1, :])
     row_z = lagrange_rows(coords[1:2, :])
@@ -509,12 +514,13 @@
     send_faces(1)
     for c in range(3):
         field[2, c] = local[1, c]
-    lines_rows = jnp.concatenate([lines_mass, lines[1] / height], axis=1)
+    loaded("words", "weights")
+    lines_rows = jnp.concatenate([lines_mass, lines_stiff], axis=1)
     ends = [lines_rows[0:1], lines_rows[length_y - 1 : length_y]]
     once = [(end[:, :length_y], end[:, length_y:]) for end in ends]
     twice = dot3(
         split(jnp.concatenate([once[0][0], once[0][1], once[1][0], once[1][1]] * 2, axis=0)),
-        (lines_hi, lines_lo),
+        split(lines_rows),
         NN,
     )
     one_lane = lax.broadcasted_iota(jnp.int32, (1, length_y), 1)
@@ -537,8 +543,8 @@
             images.append(jnp.broadcast_to(image, (length_z, 3 * length_y)))
         images.append(jnp.zeros((128 - 7 * length_z, 3 * length_y), F32))
     images = split(jnp.concatenate(images, axis=0))
-    words_x_parts = split(words_x[...])
-    words_z_parts = split(words_z[...])
+    words_x_parts = (words[0, :, : reach * length_x], words[1, :, : reach * length_x])
+    words_z_parts = (words[2], words[3])
 
     settle(pull_ss, pull_rs, pull_got.at[pl.ds(0, len(offsets))])
     small_lane = lax.broadcasted_iota(jnp.int32, (8, 128), 1) // length_z
@@ -611,13 +617,17 @@
     for newest in range(3):
         inner_products(newest)
     for c in range(3):
-        inner(6, c, field[2, c] * columns[2] * local[2, c])
+        inner(6, c, field[2, c] * columns[3] * local[2, c])
 
     total_rows = parts.shape[0]
     r_iota = lax.broadcasted_iota(jnp.int32, (total_rows, 128), 0)
     l_iota = lax.broadcasted_iota(jnp.int32, (total_rows, 128), 1)
     diagonal = r_iota == l_iota
-    summed = jnp.sum(parts[...], axis=1, keepdims=True)
+    end_lane = lax.broadcasted_iota(jnp.int32, (total_rows, 128), 1)
+    shared = jnp.logical_or(end_lane % 8 == 0, end_lane % 8 == 7)
+    tips = jnp.logical_or(end_lane == 0, end_lane == length_y - 1)
+    weight_y = jnp.where(jnp.logical_and(shared, jnp.logical_not(tips)), 0.5, 1.0)
+    summed = jnp.sum(parts[...] * weight_y, axis=1, keepdims=True)
     row = jnp.sum(jnp.where(diagonal, summed, 0.0), axis=0, keepdims=True)
 
     def gather_sum(stage, row, count, got, ss, rs, place):
@@ -682,8 +692,7 @@
     length_x, length_z, length_y = sizes
     rows = length_x * length_z
     points = owner_device.shape[0]
-    both, lines, columns, words_x, words_z = tables(*sizes)
-    plane_hi, plane_lo = split_np(both)
+    plane, lines, columns, words_x, words_z = tables(*sizes)
     every = n_wall * n_span
     first = every if every <= SINGLE_STAGE else n_wall
     faces = -(-(6 * (length_x + length_z) + 12) // 8) * 8
@@ -696,12 +705,10 @@
         owner_element.reshape(1, -1),
         ref_coords,
         roughness.reshape(1, -1),
-        plane_hi,
-        plane_lo,
+        jnp.stack(split_np(plane)),
         jnp.asarray(lines, F32),
         jnp.asarray(columns, F32),
-        jnp.asarray(words_x, F32),
-        jnp.asarray(words_z, F32),
+        jnp.stack(split_np(words_x) + split_np(words_z)),
     )
     dma = pltpu.SemaphoreType.DMA
     field, factors, neumann = pl.pallas_call(
@@ -711,11 +718,11 @@
             pltpu.VMEM((3, 8, 128), F32),
             pltpu.VMEM((2, points), F32),
         ),
-        in_specs=[hbm] * 12,
+        in_specs=[hbm] * 10,
         out_specs=(vmem, vmem, vmem),
         scratch_shapes=[pltpu.VMEM(value.shape, value.dtype) for value in operands]
         + [
-            dma((12,)),
+            dma((11,)),
             pltpu.VMEM((2, 64, length_y), F32),
             pltpu.VMEM((2, 2, 64, length_y), F32),
             pltpu.VMEM((3, 3, rows, length_y), F32),

time: 25.4 us -> 24.4 us (0.961)
  Pallas kernels: 24.6 us -> 23.6 us
    pallas_call x1, Pallas kernels: 23.8 us -> 22.8 us  [body(): pl.pallas_call(functools.partial(kernel, n_wall, n_span, sizes), out_shap...]
where the time goes in v2:
time: 24.4 us; the launch traced here: 24.2 us
  Pallas kernels  23.6 us (97%)
  between operations  0.64 us (3%)
    pallas_call x1, Pallas kernels, body(): pl.pallas_call(functools.partial(kernel, n_wall, n_span, sizes), out_shap...  22.8 us
    pallas_call x1, Pallas kernels, body(): pl.pallas_call(combine, out_shape=(jax.ShapeDtypeStruct(velocity_old.shap...  0.8 us

profile of v2, /device:TPU:0, one launch (start us, length us, event | category | flops | bytes accessed | tf_op | source)
XLA Modules:
  0.0 24.2 jit_solution(7533134733284019822)
XLA Ops:
  0.6 22.8 %shard_map.149 = (f32[3,3,256,128]{3,2,1,0:T(8,128)S(1)}, f32[3,8,128]{2,1,0:T(8,128)S(1)}, f32[2,512]{1,0:T(2,128)S(1)}) custom-call(f32[3,16,16,128]{3,2,1,0:T(8,128)} %vel_in.1, f32[1,16]{1,0:T(1,128)} %bitcast.7, s32[1,512]{1,0:T(1,128)} %bitcast.4, s32[1,512]{1,0:T(1,128)} %bitcast.5, f32[3,512]{1,0:T(4,128)} %coords_in.1, f32[1,512]{1,0:T(1,128)} %bitcast.6, ...), custom_call_target="tpu_custom_call" | custom-call | tf_op jit(solution)/shard_map/pallas_call | solution.py:714
  23.4 0.8 %shard_map.150 = (f32[3,16,16,128]{3,2,1,0:T(8,128)}, f32[2,512]{1,0:T(2,128)}) custom-call(f32[3,3,256,128]{3,2,1,0:T(8,128)S(1)} %get-tuple-element.5.field, f32[3,8,128]{2,1,0:T(8,128)S(1)} %get-tuple-element.6.factors, f32[2,512]{1,0:T(2,128)S(1)} %get-tuple-element.7.neumann_in), custom_call_target="tpu_custom_call" | custom-call | tf_op jit(solution)/shard_map/pallas_call | solution.py:752

commit v3 on v2

--- a/solution.py
+++ b/solution.py
@@ -251,6 +251,8 @@
     wall_rs,
     span_ss,
     span_rs,
+    step_one,
+    step_two,
 ):
     length_x, length_z, length_y = sizes
     rows = length_x * length_z
@@ -287,7 +289,11 @@
             loads[name].wait()
 
     single = n_wall * n_span <= SINGLE_STAGE
-    if single:
+    stepwise = single and 3 <= n_wall <= 4 * REACH and 3 <= n_span <= 4 * REACH
+    sides = ((1, 0), (-1, 0), (0, 1), (0, -1))
+    if stepwise:
+        greeted = sides
+    elif single:
         greeted = [divmod(k, n_span) for k in range(1, n_wall * n_span)]
     else:
         greeted = [(k, 0) for k in range(1, n_wall)] + [(0, k) for k in range(1, n_span)]
@@ -301,8 +307,12 @@
             - set(greeted)
         )
     barrier = pltpu.get_barrier_semaphore()
-    for dx, dz in greeted:
-        pl.semaphore_signal(barrier, inc=1, device_id=at(dx, dz), device_id_type=MESH)
+
+    def greet(semaphore, places):
+        for dx, dz in places:
+            pl.semaphore_signal(semaphore, inc=1, device_id=at(dx, dz), device_id_type=MESH)
+
+    greet(barrier, greeted)
 
     loaded("vel")
     lane = lax.broadcasted_iota(jnp.int32, (64, length_y), 1)
@@ -315,6 +325,30 @@
             moved = pltpu.roll(block, (group * 32 + 16) % length_y, 1)
             packed = jnp.where(lane // 32 == group, moved, packed)
         near[index] = packed
+    def remote(src, dst, ss, rs, where):
+        return pltpu.make_async_remote_copy(
+            src_ref=src,
+            dst_ref=dst,
+            send_sem=ss,
+            recv_sem=rs,
+            device_id=where,
+            device_id_type=MESH,
+        )
+
+    near_copies = []
+    for slot, dx in enumerate((1, -1)):
+        copy = remote(near, near_got.at[slot], near_ss, near_rs, at(dx, 0))
+        near_copies.append(copy)
+
+    def enter():
+        pl.semaphore_wait(barrier, len(greeted))
+        for copy in near_copies:
+            copy.start()
+        if stepwise:
+            greet(step_one, sides)
+
+    if stepwise:
+        enter()
     loaded("heights", "lines", "scale", "plane")
 
     layer_of = lax.broadcasted_iota(jnp.int32, (length_y, count_y), 0) // 8
@@ -339,18 +373,8 @@
     for c in range(3):
         field[0, c] = vel[c].reshape(rows, length_y) * scale
 
-    def remote(src, dst, ss, rs, where):
-        return pltpu.make_async_remote_copy(
-            src_ref=src,
-            dst_ref=dst,
-            send_sem=ss,
-            recv_sem=rs,
-            device_id=where,
-            device_id_type=MESH,
-        )
-
     face_rows = []
-    for slot, (dx, dz) in enumerate(((1, 0), (-1, 0), (0, 1), (0, -1)) + DIRS):
+    for slot, (dx, dz) in enumerate(DIRS + ((0, 1), (0, -1), (1, 0), (-1, 0))):
         size = 3 * (1 if dx and dz else length_z if dx else length_x)
         face_rows.append((sum(entry[1] for entry in face_rows), size, dx, dz))
     face_total = sum(entry[1] for entry in face_rows)
@@ -373,10 +397,11 @@
             for slot, (_, _, dx, dz) in enumerate(face_rows):
                 packed_rows, rows_of = face_part(slot, c, dx, dz)
                 face_send[turn, packed_rows, :] = local[turn, c, rows_of, :]
-        if turn == 0:
-            pl.semaphore_wait(barrier, len(greeted))
-            for copy in near_copies:
-                copy.start()
+        if turn == 0 and stepwise:
+            pl.semaphore_wait(step_one, len(sides))
+            greet(step_two, sides + DIRS)
+        elif turn == 0:
+            enter()
         for first, size, dx, dz in face_rows:
             part = (turn, pl.ds(first, size), slice(None))
             remote(
@@ -429,11 +454,6 @@
             weighted = field[newest, c] * columns[2]
             for other in range(newest + 1):
                 inner(slots[(other, newest)], c, weighted * field[other, c])
-
-    near_copies = []
-    for slot, dx in enumerate((1, -1)):
-        copy = remote(near, near_got.at[slot], near_ss, near_rs, at(dx, 0))
-        near_copies.append(copy)
 
     operate(0, 0)
     send_faces(0)
@@ -497,6 +517,8 @@
     for tile in range(1, tiles):
         bundle = bundle + pltpu.roll(flat[tile * 8 : tile * 8 + 8], tile * length_z, 1)
     pull_send[...] = bundle
+    if stepwise:
+        pl.semaphore_wait(step_two, len(sides + DIRS))
     reach = 2 * REACH + 1
     folded = n_span == 2 * REACH
     offsets = [
@@ -744,6 +766,8 @@
             dma,
             dma,
             dma,
+            pltpu.SemaphoreType.REGULAR,
+            pltpu.SemaphoreType.REGULAR,
         ],
         compiler_params=pltpu.CompilerParams(
             collective_id=0, has_side_effects=True, vmem_limit_bytes=VMEM_LIMIT

time: 24.4 us -> 23.7 us (0.971)
  Pallas kernels: 23.6 us -> 22.9 us
    pallas_call x1, Pallas kernels: 22.8 us -> 22.1 us  [body(): pl.pallas_call(functools.partial(kernel, n_wall, n_span, sizes), out_shap...]
where the time goes in v3:
time: 23.7 us; the launch traced here: 23.5 us
  Pallas kernels  22.9 us (97%)
  between operations  0.64 us (3%)
    pallas_call x1, Pallas kernels, body(): pl.pallas_call(functools.partial(kernel, n_wall, n_span, sizes), out_shap...  22.1 us
    pallas_call x1, Pallas kernels, body(): pl.pallas_call(combine, out_shape=(jax.ShapeDtypeStruct(velocity_old.shap...  0.8 us

profile of v3, /device:TPU:0, one launch (start us, length us, event | category | flops | bytes accessed | tf_op | source)
XLA Modules:
  0.0 23.5 jit_solution(11511686265980209408)
XLA Ops:
  0.6 22.1 %shard_map.149 = (f32[3,3,256,128]{3,2,1,0:T(8,128)S(1)}, f32[3,8,128]{2,1,0:T(8,128)S(1)}, f32[2,512]{1,0:T(2,128)S(1)}) custom-call(f32[3,16,16,128]{3,2,1,0:T(8,128)} %vel_in.1, f32[1,16]{1,0:T(1,128)} %bitcast.7, s32[1,512]{1,0:T(1,128)} %bitcast.4, s32[1,512]{1,0:T(1,128)} %bitcast.5, f32[3,512]{1,0:T(4,128)} %coords_in.1, f32[1,512]{1,0:T(1,128)} %bitcast.6, ...), custom_call_target="tpu_custom_call" | custom-call | tf_op jit(solution)/shard_map/pallas_call | solution.py:736
  22.7 0.8 %shard_map.150 = (f32[3,16,16,128]{3,2,1,0:T(8,128)}, f32[2,512]{1,0:T(2,128)}) custom-call(f32[3,3,256,128]{3,2,1,0:T(8,128)S(1)} %get-tuple-element.5.field, f32[3,8,128]{2,1,0:T(8,128)S(1)} %get-tuple-element.6.factors, f32[2,512]{1,0:T(2,128)S(1)} %get-tuple-element.7.neumann_in), custom_call_target="tpu_custom_call" | custom-call | tf_op jit(solution)/shard_map/pallas_call | solution.py:776

commit v4 on v3

--- a/solution.py
+++ b/solution.py
@@ -163,11 +163,21 @@
 
     words_x = words(length_x, mass_x, stiffness * (2.0 / element_dx), 0.0)
     words_z = words(length_z, mass_z, stiffness * (2.0 / element_dz), inverse_step)
-    pad = np.zeros((128, 128 - reach * length_z))
-    words_z = np.concatenate([words_z, pad], axis=1)
-    pad = np.zeros((128, 128 - reach * length_x))
-    words_x = np.concatenate([words_x, pad], axis=1)
-    return plane, lines, columns, words_x, words_z
+    full = range(REACH - 1, REACH + 2)
+    half = 4 * length_x
+    turned = words_z.T
+    along_z = np.concatenate(
+        [np.tile(turned[iz * length_z : (iz + 1) * length_z], (8, 1)) for iz in full]
+        + [np.tile(turned[row : row + 1], (half, 1)) for row in (2 * REACH * length_z, length_z - 1)],
+        axis=0,
+    )
+    ends = [2 * REACH * length_x] * 4 + [length_x - 1] * 4
+    along_x = np.concatenate(
+        [words_x[:, (REACH - 1) * length_x : (REACH + 2) * length_x], words_x[:, ends]]
+        + [np.zeros((128, 8))],
+        axis=1,
+    )
+    return plane, lines, columns, along_x, along_z
 
 
 def split(value):
@@ -215,7 +225,8 @@
     plane_in,
     lines_in,
     columns_in,
-    words_in,
+    along_x_in,
+    along_z_in,
     field,
     factors,
     neumann,
@@ -228,7 +239,8 @@
     sheet,
     lines,
     columns,
-    words,
+    along_x,
+    along_z,
     load_sem,
     near,
     near_got,
@@ -240,6 +252,7 @@
     wall_got,
     span_got,
     pull_send,
+    edge_send,
     pull_got,
     pull_ss,
     pull_rs,
@@ -276,7 +289,8 @@
                 ("owner", owner_in, owner),
                 ("element", element_in, element),
                 ("roughness", roughness_in, roughness),
-                ("words", words_in, words),
+                ("along_x", along_x_in, along_x),
+                ("along_z", along_z_in, along_z),
                 ("weights", columns_in.at[pl.ds(2, 2)], columns.at[pl.ds(2, 2)]),
             )
         )
@@ -290,9 +304,9 @@
 
     single = n_wall * n_span <= SINGLE_STAGE
     stepwise = single and 3 <= n_wall <= 4 * REACH and 3 <= n_span <= 4 * REACH
-    sides = ((1, 0), (-1, 0), (0, 1), (0, -1))
+    across_wall = ((1, 0), (-1, 0))
     if stepwise:
-        greeted = sides
+        greeted = across_wall + tuple((0, k) for k in range(1, n_span))
     elif single:
         greeted = [divmod(k, n_span) for k in range(1, n_wall * n_span)]
     else:
@@ -345,7 +359,7 @@
         for copy in near_copies:
             copy.start()
         if stepwise:
-            greet(step_one, sides)
+            greet(step_one, across_wall)
 
     if stepwise:
         enter()
@@ -397,16 +411,23 @@
             for slot, (_, _, dx, dz) in enumerate(face_rows):
                 packed_rows, rows_of = face_part(slot, c, dx, dz)
                 face_send[turn, packed_rows, :] = local[turn, c, rows_of, :]
-        if turn == 0 and stepwise:
-            pl.semaphore_wait(step_one, len(sides))
-            greet(step_two, sides + DIRS)
-        elif turn == 0:
+        first_turn = turn == 0 and stepwise
+        if turn == 0 and not stepwise:
             enter()
-        for first, size, dx, dz in face_rows:
-            part = (turn, pl.ds(first, size), slice(None))
-            remote(
-                face_send.at[part], face_got.at[part], face_ss.at[turn], face_rs.at[turn], at(dx, dz)
-            ).start()
+        for corners in (False, True) if first_turn else (True, False):
+            if corners and first_turn:
+                pl.semaphore_wait(step_one, len(across_wall))
+                greet(step_two, across_wall)
+            for first, size, dx, dz in face_rows:
+                if bool(dx and dz) == corners:
+                    part = (turn, pl.ds(first, size), slice(None))
+                    remote(
+                        face_send.at[part],
+                        face_got.at[part],
+                        face_ss.at[turn],
+                        face_rs.at[turn],
+                        at(dx, dz),
+                    ).start()
 
     def settle(ss, rs, ref):
         for semaphore in (rs, ss):
@@ -505,38 +526,62 @@
     node = lax.broadcasted_iota(jnp.int32, (length_x, rows), 1) // length_z
     node_row = lax.broadcasted_iota(jnp.int32, (length_x, rows), 0)
     masked = jnp.concatenate([jnp.where(node == node_row, plane, 0.0) for plane in planes], axis=0)
-    pick_row = lax.broadcasted_iota(jnp.int32, (rows, 128), 0)
-    pick_lane = lax.broadcasted_iota(jnp.int32, (rows, 128), 1)
-    pick = jnp.where(lax.rem(pick_row, length_z) == pick_lane, 1.0, 0.0).astype(BF16)
+    pick_row = lax.rem(lax.broadcasted_iota(jnp.int32, (rows, 256), 0), length_z)
+    pick_lane = lax.broadcasted_iota(jnp.int32, (rows, 256), 1)
+    wanted_z = jnp.where(
+        pick_lane < 128, lax.rem(pick_lane, length_z), (length_z - 1) * ((pick_lane - 128) // 64)
+    )
+    pick = jnp.where(pick_row == wanted_z, 1.0, 0.0).astype(BF16)
     masked_hi, masked_lo = split(masked)
     flat = jnp.dot(masked_hi, pick, preferred_element_type=F32) + jnp.dot(
         masked_lo, pick, preferred_element_type=F32
     )
-    bundle = flat[0:8]
     tiles = 4 * length_x // 8
-    for tile in range(1, tiles):
-        bundle = bundle + pltpu.roll(flat[tile * 8 : tile * 8 + 8], tile * length_z, 1)
+    tile_lane = lax.broadcasted_iota(jnp.int32, (8, 128), 1)
+    tile_row = lax.broadcasted_iota(jnp.int32, (8, 128), 0)
+    block_of = tile_lane // length_z
+    bundle = jnp.zeros((8, 128), F32)
+    for tile in range(tiles):
+        bundle = jnp.where(block_of == tile, flat[tile * 8 : tile * 8 + 8, :128], bundle)
     pull_send[...] = bundle
+    flat_row = lax.broadcasted_iota(jnp.int32, (64, 128), 0)
+    flat_lane = lax.broadcasted_iota(jnp.int32, (64, 128), 1)
+    ends_x = lax.rem(flat_lane, 64) // length_z * length_x + (length_x - 1) * (flat_lane // 64)
+    edge_send[0:1, :] = jnp.sum(
+        jnp.where(lax.rem(flat_lane, 64) == flat_row, flat[:, 128:], 0.0), axis=0, keepdims=True
+    )
+    edge_send[1:2, :] = jnp.sum(
+        jnp.where(flat_row == ends_x, flat[:, :128], 0.0), axis=0, keepdims=True
+    )
     if stepwise:
-        pl.semaphore_wait(step_two, len(sides + DIRS))
+        pl.semaphore_wait(step_two, len(across_wall))
     reach = 2 * REACH + 1
-    folded = n_span == 2 * REACH
     offsets = [
         (dx, dz)
         for dx in range(-REACH, REACH + 1)
         for dz in range(-REACH, REACH + 1)
-        if (dx, dz) != (0, 0) and not (folded and dz == REACH)
+        if (dx, dz) != (0, 0)
     ]
+    nearby = [place for place in offsets if max(abs(place[0]), abs(place[1])) < REACH]
+    remaining = [place for place in offsets if place not in nearby]
+    pull_rows = {place: pl.ds(8 * index, 8) for index, place in enumerate(nearby)}
+    for index, place in enumerate(remaining):
+        pull_rows[place] = pl.ds(8 * len(nearby) + index, 1)
     for dx, dz in sorted(offsets, key=lambda pair: -abs(pair[0]) - abs(pair[1])):
-        slot = (REACH - dx) * reach + (REACH - dz)
-        remote(pull_send, pull_got.at[slot], pull_ss, pull_rs, at(dx, dz)).start()
+        if (dx, dz) in nearby:
+            source = pull_send
+        else:
+            source = edge_send.at[pl.ds(0 if abs(dz) == REACH else 1, 1), :]
+        remote(
+            source, pull_got.at[pull_rows[(-dx, -dz)], :], pull_ss, pull_rs, at(dx, dz)
+        ).start()
 
     add_faces(0)
     operate(1, 1)
     send_faces(1)
     for c in range(3):
         field[2, c] = local[1, c]
-    loaded("words", "weights")
+    loaded("along_x", "along_z", "weights")
     lines_rows = jnp.concatenate([lines_mass, lines_stiff], axis=1)
     ends = [lines_rows[0:1], lines_rows[length_y - 1 : length_y]]
     once = [(end[:, :length_y], end[:, length_y:]) for end in ends]
@@ -549,58 +594,75 @@
     zero = jnp.zeros((1, length_y), F32)
     images = []
     for side in range(2):
-        tip = jnp.where(one_lane == side * (length_y - 1), 1.0, 0.0)
         by_mass, by_stiff = twice[2 * side : 2 * side + 1], twice[2 * side + 1 : 2 * side + 2]
+        moved_tip = jnp.where(one_lane == length_y // 2 - side, 1.0, 0.0)
         rows_of = [
-            (tip, zero, zero),
-            (zero, once[side][0], zero),
-            (zero, once[side][1], zero),
-            (zero, zero, by_mass[:, :length_y]),
-            (zero, zero, by_stiff[:, :length_y]),
-            (zero, zero, by_mass[:, length_y:]),
-            (zero, zero, by_stiff[:, length_y:]),
+            (zero, moved_tip),
+            (zero, once[side][0]),
+            (zero, once[side][1]),
+            (by_mass[:, :length_y], zero),
+            (by_stiff[:, :length_y], zero),
+            (by_mass[:, length_y:], zero),
+            (by_stiff[:, length_y:], zero),
         ]
         for entry in rows_of:
             image = jnp.concatenate(entry, axis=1)
-            images.append(jnp.broadcast_to(image, (length_z, 3 * length_y)))
-        images.append(jnp.zeros((128 - 7 * length_z, 3 * length_y), F32))
+            images.append(jnp.broadcast_to(image, (length_z, 2 * length_y)))
+        images.append(jnp.zeros((128 - 7 * length_z, 2 * length_y), F32))
     images = split(jnp.concatenate(images, axis=0))
-    words_x_parts = (words[0, :, : reach * length_x], words[1, :, : reach * length_x])
-    words_z_parts = (words[2], words[3])
-
-    settle(pull_ss, pull_rs, pull_got.at[pl.ds(0, len(offsets))])
-    small_lane = lax.broadcasted_iota(jnp.int32, (8, 128), 1) // length_z
+    settle(pull_ss, pull_rs, pull_got)
+    low_half = tile_lane < 64
+    low_rows = tile_row < 4
+
+    def edge(dx, dz):
+        return jnp.broadcast_to(pull_got[pull_rows[(dx, dz)], :], (8, 128))
+
+    def both_ends(dx):
+        return jnp.where(low_half, edge(dx, REACH), edge(dx, -REACH))
+
+    middle = range(-REACH + 1, REACH)
     spans = []
-    for ix in range(reach):
-        pieces = [
-            bundle
-            if (ix, iz) == (REACH, REACH)
-            else pull_got[ix * reach + (reach - 1 if folded and iz == 0 else iz)]
-            for iz in range(reach)
-        ]
+    for dx in middle:
+        ends = both_ends(dx)
+        parts_z = [bundle if (dx, dz) == (0, 0) else pull_got[pull_rows[(dx, dz)], :] for dz in middle]
         for tile in range(tiles):
-            line = jnp.zeros((8, 128), F32)
-            for iz in range(reach):
-                shift = ((iz - tile) * length_z) % 128
-                moved = pltpu.roll(pieces[iz], shift, 1) if shift else pieces[iz]
-                line = jnp.where(small_lane == iz, moved, line)
-            spans.append(line)
-    along_z = dot3(split(jnp.concatenate(spans, axis=0)), words_z_parts, NT)
+            pieces = [jnp.where(block_of == tile, part, 0.0) for part in parts_z]
+            pieces.append(jnp.where(lax.rem(tile_lane, 64) == tile_row + 8 * tile, ends, 0.0))
+            spans.append(jnp.concatenate(pieces, axis=1))
+    pieces = [
+        jnp.where(block_of == tile_row, jnp.where(low_rows, edge(REACH, dz), edge(-REACH, dz)), 0.0)
+        for dz in middle
+    ]
+    corner_lane = lax.rem(tile_row, 4) * length_x + (length_x - 1) * (tile_row // 4)
+    ends = jnp.where(low_rows, both_ends(REACH), both_ends(-REACH))
+    pieces.append(jnp.where(lax.rem(tile_lane, 64) == corner_lane, ends, 0.0))
+    spans.append(jnp.concatenate(pieces, axis=1))
+    spans.append(jnp.zeros((8, 512), F32))
+    spans_hi, spans_lo = split(jnp.concatenate(spans, axis=0))
+    reached = jnp.dot(spans_hi, along_z[...], preferred_element_type=F32)
+    reached = (reached[:, :128] + reached[:, 128:]) + jnp.dot(
+        spans_lo, along_z[:, :128], preferred_element_type=F32
+    )
     by_plane = []
     for plane in range(4):
-        by_plane.append(
-            jnp.concatenate(
-                [
-                    along_z[(ix * 4 + plane) * length_x : (ix * 4 + plane + 1) * length_x]
-                    for ix in range(reach)
-                ],
-                axis=0,
-            )
-        )
-    both_ways = dot3(words_x_parts, split(jnp.concatenate(by_plane, axis=1)), NN)
+        kept = [
+            reached[ix * 64 + plane * length_x : ix * 64 + (plane + 1) * length_x]
+            for ix in range(len(middle))
+        ]
+        last = reached[64 * len(middle) : 64 * len(middle) + 8]
+        kept.append(jnp.where(lax.rem(tile_row, 4) == plane, last, 0.0))
+        kept.append(jnp.zeros((8, 128), F32))
+        by_plane.append(jnp.concatenate(kept, axis=0))
+    stacked_hi, stacked_lo = split(jnp.concatenate(by_plane, axis=1))
+    both_ways = jnp.dot(
+        along_x[...],
+        jnp.concatenate([stacked_hi, stacked_lo, stacked_hi], axis=0),
+        preferred_element_type=F32,
+    )
     block_lane = lax.broadcasted_iota(jnp.int32, (length_x, 128), 1) // length_z
     keep_row = lax.rem(lax.broadcasted_iota(jnp.int32, (rows, 256), 0), length_z)
     keep_lane = lax.rem(lax.broadcasted_iota(jnp.int32, (rows, 256), 1), length_z)
+    wall_lane = lax.broadcasted_iota(jnp.int32, (rows, length_y), 1)
     tractions = []
     for index in range(2):
         blocks = []
@@ -620,17 +682,20 @@
             [jnp.broadcast_to(wide[x : x + 1], (length_z, 256)) for x in range(length_x)], axis=0
         )
         tall = jnp.where(keep_row == keep_lane, tall, 0.0)
-        tractions.append(dot3(split(tall), images, NN))
+        deep = dot3(split(tall), images, NN)
+        level_two, shallow = deep[:, :length_y], deep[:, length_y:]
+        tip = jnp.logical_or(wall_lane == 0, wall_lane == length_y - 1)
+        level_zero = jnp.where(tip, pltpu.roll(shallow, length_y // 2, 1), 0.0)
+        outside = jnp.logical_or(wall_lane < length_y // 4, wall_lane >= 3 * length_y // 4)
+        level_one = jnp.where(outside, shallow, 0.0)
+        tractions.append((level_zero, level_one, level_two))
     add_faces(1)
     t1, t2 = shifts
     for c in range(3):
         chain = [field[level, c] for level in range(3)]
         if c != 1:
             taus = tractions[c // 2]
-            chain = [
-                chain[level] + taus[:, level * length_y : (level + 1) * length_y]
-                for level in range(3)
-            ]
+            chain = [chain[level] + taus[level] for level in range(3)]
         v1 = chain[1] - t1 * chain[0]
         field[0, c] = chain[0]
         field[1, c] = v1
@@ -714,7 +779,8 @@
     length_x, length_z, length_y = sizes
     rows = length_x * length_z
     points = owner_device.shape[0]
-    plane, lines, columns, words_x, words_z = tables(*sizes)
+    plane, lines, columns, along_x, along_z = tables(*sizes)
+    along_x_hi, along_x_lo = split_np(along_x)
     every = n_wall * n_span
     first = every if every <= SINGLE_STAGE else n_wall
     faces = -(-(6 * (length_x + length_z) + 12) // 8) * 8
@@ -730,7 +796,8 @@
         jnp.stack(split_np(plane)),
         jnp.asarray(lines, F32),
         jnp.asarray(columns, F32),
-        jnp.stack(split_np(words_x) + split_np(words_z)),
+        jnp.concatenate([along_x_hi, along_x_hi, along_x_lo], axis=1),
+        jnp.concatenate(split_np(along_z), axis=1),
     )
     dma = pltpu.SemaphoreType.DMA
     field, factors, neumann = pl.pallas_call(
@@ -740,11 +807,11 @@
             pltpu.VMEM((3, 8, 128), F32),
             pltpu.VMEM((2, points), F32),
         ),
-        in_specs=[hbm] * 10,
+        in_specs=[hbm] * 11,
         out_specs=(vmem, vmem, vmem),
         scratch_shapes=[pltpu.VMEM(value.shape, value.dtype) for value in operands]
         + [
-            dma((11,)),
+            dma((12,)),
             pltpu.VMEM((2, 64, length_y), F32),
             pltpu.VMEM((2, 2, 64, length_y), F32),
             pltpu.VMEM((3, 3, rows, length_y), F32),
@@ -755,7 +822,8 @@
             pltpu.VMEM((first - 1, 128), F32),
             pltpu.VMEM((n_span - 1, 128), F32),
             pltpu.VMEM((8, 128), F32),
-            pltpu.VMEM((25, 8, 128), F32),
+            pltpu.VMEM((8, 128), F32),
+            pltpu.VMEM((80, 128), F32),
             dma,
             dma,
             dma,

time: 23.7 us -> 22.2 us (0.937)
  Pallas kernels: 22.9 us -> 21.4 us
    pallas_call x1, Pallas kernels: 22.1 us -> 20.6 us  [body(): pl.pallas_call(functools.partial(kernel, n_wall, n_span, sizes), out_shap...]
where the time goes in v4:
time: 22.2 us; the launch traced here: 22 us
  Pallas kernels  21.4 us (96%)
  between operations  0.64 us (3%)
    pallas_call x1, Pallas kernels, body(): pl.pallas_call(functools.partial(kernel, n_wall, n_span, sizes), out_shap...  20.6 us
    pallas_call x1, Pallas kernels, body(): pl.pallas_call(combine, out_shape=(jax.ShapeDtypeStruct(velocity_old.shap...  0.8 us

profile of v4, /device:TPU:0, one launch (start us, length us, event | category | flops | bytes accessed | tf_op | source)
XLA Modules:
  0.0 22.0 jit_solution(14411482359948973249)
XLA Ops:
  0.6 20.6 %shard_map.149 = (f32[3,3,256,128]{3,2,1,0:T(8,128)S(1)}, f32[3,8,128]{2,1,0:T(8,128)S(1)}, f32[2,512]{1,0:T(2,128)S(1)}) custom-call(f32[3,16,16,128]{3,2,1,0:T(8,128)} %vel_in.1, f32[1,16]{1,0:T(1,128)} %bitcast.7, s32[1,512]{1,0:T(1,128)} %bitcast.4, s32[1,512]{1,0:T(1,128)} %bitcast.5, f32[3,512]{1,0:T(4,128)} %coords_in.1, f32[1,512]{1,0:T(1,128)} %bitcast.6, ...), custom_call_target="tpu_custom_call" | custom-call | tf_op jit(solution)/shard_map/pallas_call | solution.py:803
  21.2 0.8 %shard_map.150 = (f32[3,16,16,128]{3,2,1,0:T(8,128)}, f32[2,512]{1,0:T(2,128)}) custom-call(f32[3,3,256,128]{3,2,1,0:T(8,128)S(1)} %get-tuple-element.5.field, f32[3,8,128]{2,1,0:T(8,128)S(1)} %get-tuple-element.6.factors, f32[2,512]{1,0:T(2,128)S(1)} %get-tuple-element.7.neumann_in), custom_call_target="tpu_custom_call" | custom-call | tf_op jit(solution)/shard_map/pallas_call | solution.py:844

commit v5 on v4

--- a/solution.py
+++ b/solution.py
@@ -502,6 +502,9 @@
     along = jnp.where(wanted, jnp.concatenate([row_y] * (length_y // 8), axis=0), 0.0)
     spread = split(spread)
 
+    drag = karman / jnp.log(sample_height / roughness[...])
+    drag = drag * drag * (-1.0 / viscosity)
+
     settle(near_ss, near_rs, near_got)
 
     sampled = []
@@ -513,8 +516,7 @@
         sampled.append(jnp.sum(values * along, axis=0, keepdims=True))
     stream, spanwise = sampled
     speed = jnp.sqrt(stream * stream + spanwise * spanwise + speed_floor)
-    drag = karman / jnp.log(sample_height / roughness[...])
-    factor = -(drag * drag * speed / viscosity)
+    factor = drag * speed
     gradient = (factor * stream, factor * spanwise)
     neumann[0:1, :] = gradient[0]
     neumann[1:2, :] = gradient[1]
@@ -689,7 +691,6 @@
         outside = jnp.logical_or(wall_lane < length_y // 4, wall_lane >= 3 * length_y // 4)
         level_one = jnp.where(outside, shallow, 0.0)
         tractions.append((level_zero, level_one, level_two))
-    add_faces(1)
     t1, t2 = shifts
     for c in range(3):
         chain = [field[level, c] for level in range(3)]
@@ -700,11 +701,25 @@
         field[0, c] = chain[0]
         field[1, c] = v1
         field[2, c] = chain[2] - t1 * chain[1] - t2 * v1
-    operate(2, 2)
-    for newest in range(3):
+    for newest in range(2):
         inner_products(newest)
+    add_faces(1)
+    highs = [field[2, c].astype(BF16) for c in range(3)]
+    along_y = jnp.dot(
+        jnp.concatenate(highs, axis=0), lines_packed[:length_y], preferred_element_type=F32
+    )
+    wide = jnp.concatenate(highs, axis=1)
+    across = jnp.dot(sheet[0], wide, preferred_element_type=F32)
+    across_low = jnp.dot(sheet[1], wide, preferred_element_type=F32)
+    inner_products(2)
     for c in range(3):
-        inner(6, c, field[2, c] * columns[3] * local[2, c])
+        here = slice(c * length_y, (c + 1) * length_y)
+        tall = along_y[c * rows : (c + 1) * rows]
+        tall = tall[:, :length_y] + tall[:, length_y:]
+        image = (across[:, here] + across_low[:, here]) * mass_row + tall * columns[1]
+        value = field[2, c]
+        partner = value + (value - highs[c].astype(F32))
+        inner(6, c, partner * columns[3] * image)
 
     total_rows = parts.shape[0]
     r_iota = lax.broadcasted_iota(jnp.int32, (total_rows, 128), 0)
@@ -814,7 +829,7 @@
             dma((12,)),
             pltpu.VMEM((2, 64, length_y), F32),
             pltpu.VMEM((2, 2, 64, length_y), F32),
-            pltpu.VMEM((3, 3, rows, length_y), F32),
+            pltpu.VMEM((ROUNDS, 3, rows, length_y), F32),
             pltpu.VMEM((ROUNDS, faces, length_y), F32),
             pltpu.VMEM((ROUNDS, faces, length_y), F32),
             pltpu.VMEM((56, length_y), F32),

time: 22.2 us -> 21.8 us (0.982)
  Pallas kernels: 21.4 us -> 21 us
    pallas_call x1, Pallas kernels: 20.6 us -> 20.2 us  [body(): pl.pallas_call(functools.partial(kernel, n_wall, n_span, sizes), out_shap...]
where the time goes in v5:
time: 21.8 us; the launch traced here: 21.7 us
  Pallas kernels  21 us (96%)
  between operations  0.64 us (3%)
    pallas_call x1, Pallas kernels, body(): pl.pallas_call(functools.partial(kernel, n_wall, n_span, sizes), out_shap...  20.2 us
    pallas_call x1, Pallas kernels, body(): pl.pallas_call(combine, out_shape=(jax.ShapeDtypeStruct(velocity_old.shap...  0.8 us

profile of v5, /device:TPU:0, one launch (start us, length us, event | category | flops | bytes accessed | tf_op | source)
XLA Modules:
  0.0 21.7 jit_solution(16936079011857862809)
XLA Ops:
  0.6 20.2 %shard_map.149 = (f32[3,3,256,128]{3,2,1,0:T(8,128)S(1)}, f32[3,8,128]{2,1,0:T(8,128)S(1)}, f32[2,512]{1,0:T(2,128)S(1)}) custom-call(f32[3,16,16,128]{3,2,1,0:T(8,128)} %vel_in.1, f32[1,16]{1,0:T(1,128)} %bitcast.7, s32[1,512]{1,0:T(1,128)} %bitcast.4, s32[1,512]{1,0:T(1,128)} %bitcast.5, f32[3,512]{1,0:T(4,128)} %coords_in.1, f32[1,512]{1,0:T(1,128)} %bitcast.6, ...), custom_call_target="tpu_custom_call" | custom-call | tf_op jit(solution)/shard_map/pallas_call | solution.py:818
  20.9 0.8 %shard_map.150 = (f32[3,16,16,128]{3,2,1,0:T(8,128)}, f32[2,512]{1,0:T(2,128)}) custom-call(f32[3,3,256,128]{3,2,1,0:T(8,128)S(1)} %get-tuple-element.5.field, f32[3,8,128]{2,1,0:T(8,128)S(1)} %get-tuple-element.6.factors, f32[2,512]{1,0:T(2,128)S(1)} %get-tuple-element.7.neumann_in), custom_call_target="tpu_custom_call" | custom-call | tf_op jit(solution)/shard_map/pallas_call | solution.py:859

commit v6 on v5

--- a/solution.py
+++ b/solution.py
@@ -164,16 +164,17 @@
     words_x = words(length_x, mass_x, stiffness * (2.0 / element_dx), 0.0)
     words_z = words(length_z, mass_z, stiffness * (2.0 / element_dz), inverse_step)
     full = range(REACH - 1, REACH + 2)
-    half = 4 * length_x
     turned = words_z.T
+    ends_z = [2 * REACH * length_z] * 8 + [length_z - 1] * 8
     along_z = np.concatenate(
         [np.tile(turned[iz * length_z : (iz + 1) * length_z], (8, 1)) for iz in full]
-        + [np.tile(turned[row : row + 1], (half, 1)) for row in (2 * REACH * length_z, length_z - 1)],
+        + [np.tile(turned[ends_z], (8, 1))],
         axis=0,
     )
-    ends = [2 * REACH * length_x] * 4 + [length_x - 1] * 4
+    ends = [2 * REACH * length_x, length_x - 1] * 4
+    inner = [ix * length_x + half + (-r) % 8 for ix in full for half in (0, 8) for r in range(8)]
     along_x = np.concatenate(
-        [words_x[:, (REACH - 1) * length_x : (REACH + 2) * length_x], words_x[:, ends]]
+        [words_x[:, inner], words_x[:, ends]]
         + [np.zeros((128, 8))],
         axis=1,
     )
@@ -254,18 +255,15 @@
     pull_send,
     edge_send,
     pull_got,
-    pull_ss,
+    everything,
+    sent,
+    near_rs,
     pull_rs,
-    near_ss,
-    near_rs,
-    face_ss,
     face_rs,
-    wall_ss,
     wall_rs,
-    span_ss,
-    span_rs,
     step_one,
     step_two,
+    *span_rs,
 ):
     length_x, length_z, length_y = sizes
     rows = length_x * length_z
@@ -351,7 +349,7 @@
 
     near_copies = []
     for slot, dx in enumerate((1, -1)):
-        copy = remote(near, near_got.at[slot], near_ss, near_rs, at(dx, 0))
+        copy = remote(near, near_got.at[slot], sent, near_rs, at(dx, 0))
         near_copies.append(copy)
 
     def enter():
@@ -414,27 +412,28 @@
         first_turn = turn == 0 and stepwise
         if turn == 0 and not stepwise:
             enter()
-        for corners in (False, True) if first_turn else (True, False):
-            if corners and first_turn:
+        for stage in ((0,), (2, 1)) if first_turn else ((2, 0, 1),):
+            if stage[0] == 2 and first_turn:
                 pl.semaphore_wait(step_one, len(across_wall))
                 greet(step_two, across_wall)
-            for first, size, dx, dz in face_rows:
-                if bool(dx and dz) == corners:
+            for kind in stage:
+                for first, size, dx, dz in face_rows:
+                    if (2 if dx and dz else abs(dx)) != kind:
+                        continue
                     part = (turn, pl.ds(first, size), slice(None))
                     remote(
                         face_send.at[part],
                         face_got.at[part],
-                        face_ss.at[turn],
+                        sent,
                         face_rs.at[turn],
                         at(dx, dz),
                     ).start()
 
-    def settle(ss, rs, ref):
-        for semaphore in (rs, ss):
-            pltpu.make_async_copy(ref, ref, semaphore).wait()
+    def settle(semaphore, ref):
+        pltpu.make_async_copy(ref, ref, semaphore).wait()
 
     def add_faces(turn):
-        settle(face_ss.at[turn], face_rs.at[turn], face_got.at[turn, pl.ds(0, face_total), :])
+        settle(face_rs.at[turn], face_got.at[turn, pl.ds(0, face_total), :])
         for c in range(3):
             for slot, (_, _, dx, dz) in enumerate(face_rows):
                 packed_rows, rows_of = face_part(slot, c, -dx, -dz)
@@ -505,7 +504,7 @@
     drag = karman / jnp.log(sample_height / roughness[...])
     drag = drag * drag * (-1.0 / viscosity)
 
-    settle(near_ss, near_rs, near_got)
+    settle(near_rs, near_got)
 
     sampled = []
     for index in range(2):
@@ -525,36 +524,25 @@
     for index in range(2):
         pull = viscosity * gradient[index]
         planes += [pull[:, :rows], pull[:, rows:]]
-    node = lax.broadcasted_iota(jnp.int32, (length_x, rows), 1) // length_z
-    node_row = lax.broadcasted_iota(jnp.int32, (length_x, rows), 0)
-    masked = jnp.concatenate([jnp.where(node == node_row, plane, 0.0) for plane in planes], axis=0)
-    pick_row = lax.rem(lax.broadcasted_iota(jnp.int32, (rows, 256), 0), length_z)
-    pick_lane = lax.broadcasted_iota(jnp.int32, (rows, 256), 1)
-    wanted_z = jnp.where(
-        pick_lane < 128, lax.rem(pick_lane, length_z), (length_z - 1) * ((pick_lane - 128) // 64)
-    )
-    pick = jnp.where(pick_row == wanted_z, 1.0, 0.0).astype(BF16)
-    masked_hi, masked_lo = split(masked)
-    flat = jnp.dot(masked_hi, pick, preferred_element_type=F32) + jnp.dot(
-        masked_lo, pick, preferred_element_type=F32
-    )
     tiles = 4 * length_x // 8
     tile_lane = lax.broadcasted_iota(jnp.int32, (8, 128), 1)
     tile_row = lax.broadcasted_iota(jnp.int32, (8, 128), 0)
     block_of = tile_lane // length_z
     bundle = jnp.zeros((8, 128), F32)
+    fringe = jnp.zeros((8, 128), F32)
     for tile in range(tiles):
-        bundle = jnp.where(block_of == tile, flat[tile * 8 : tile * 8 + 8, :128], bundle)
+        part = planes[tile // 2][:, 128 * (tile % 2) : 128 * (tile % 2) + 128]
+        part = jnp.broadcast_to(part, (8, 128))
+        spread_rows = pltpu.roll(part, 0, 1, stride=length_z, stride_axis=0)
+        spread_rows = pltpu.roll(spread_rows, (8 - tile) % 8, 0)
+        bundle = jnp.where(block_of == tile, spread_rows, bundle)
+        for end in range(2):
+            turned = pltpu.roll(part, 7 * (1 - end), 1, stride=length_z - 1, stride_axis=0)
+            wanted_lane = tile * length_z + 8 * end + 7 - tile_row
+            fringe = jnp.where(tile_lane == wanted_lane, turned, fringe)
     pull_send[...] = bundle
-    flat_row = lax.broadcasted_iota(jnp.int32, (64, 128), 0)
-    flat_lane = lax.broadcasted_iota(jnp.int32, (64, 128), 1)
-    ends_x = lax.rem(flat_lane, 64) // length_z * length_x + (length_x - 1) * (flat_lane // 64)
-    edge_send[0:1, :] = jnp.sum(
-        jnp.where(lax.rem(flat_lane, 64) == flat_row, flat[:, 128:], 0.0), axis=0, keepdims=True
-    )
-    edge_send[1:2, :] = jnp.sum(
-        jnp.where(flat_row == ends_x, flat[:, :128], 0.0), axis=0, keepdims=True
-    )
+    edge_send[0:1, :] = jnp.sum(fringe, axis=0, keepdims=True)
+    edge_send[1:2, :] = jnp.where(block_of[0:1] % 2 == 0, bundle[0:1], bundle[1:2])
     if stepwise:
         pl.semaphore_wait(step_two, len(across_wall))
     reach = 2 * REACH + 1
@@ -575,7 +563,7 @@
         else:
             source = edge_send.at[pl.ds(0 if abs(dz) == REACH else 1, 1), :]
         remote(
-            source, pull_got.at[pull_rows[(-dx, -dz)], :], pull_ss, pull_rs, at(dx, dz)
+            source, pull_got.at[pull_rows[(-dx, -dz)], :], sent, pull_rs, at(dx, dz)
         ).start()
 
     add_faces(0)
@@ -612,9 +600,10 @@
             images.append(jnp.broadcast_to(image, (length_z, 2 * length_y)))
         images.append(jnp.zeros((128 - 7 * length_z, 2 * length_y), F32))
     images = split(jnp.concatenate(images, axis=0))
-    settle(pull_ss, pull_rs, pull_got)
-    low_half = tile_lane < 64
-    low_rows = tile_row < 4
+    low_half = tile_lane & 8 == 0
+    low_rows = tile_row & 1 == 0
+    diagonal_of = (tile_lane + tile_row) & 7
+    settle(pull_rs, pull_got)
 
     def edge(dx, dz):
         return jnp.broadcast_to(pull_got[pull_rows[(dx, dz)], :], (8, 128))
@@ -629,15 +618,18 @@
         parts_z = [bundle if (dx, dz) == (0, 0) else pull_got[pull_rows[(dx, dz)], :] for dz in middle]
         for tile in range(tiles):
             pieces = [jnp.where(block_of == tile, part, 0.0) for part in parts_z]
-            pieces.append(jnp.where(lax.rem(tile_lane, 64) == tile_row + 8 * tile, ends, 0.0))
+            kept = jnp.logical_and(block_of == tile, diagonal_of == (7 - tile) % 8)
+            pieces.append(jnp.where(kept, ends, 0.0))
             spans.append(jnp.concatenate(pieces, axis=1))
     pieces = [
         jnp.where(block_of == tile_row, jnp.where(low_rows, edge(REACH, dz), edge(-REACH, dz)), 0.0)
         for dz in middle
     ]
-    corner_lane = lax.rem(tile_row, 4) * length_x + (length_x - 1) * (tile_row // 4)
+    kept = jnp.logical_and(
+        block_of == tile_row, (tile_lane + tile_row + (tile_row & 1)) & 7 == 7
+    )
     ends = jnp.where(low_rows, both_ends(REACH), both_ends(-REACH))
-    pieces.append(jnp.where(lax.rem(tile_lane, 64) == corner_lane, ends, 0.0))
+    pieces.append(jnp.where(kept, ends, 0.0))
     spans.append(jnp.concatenate(pieces, axis=1))
     spans.append(jnp.zeros((8, 512), F32))
     spans_hi, spans_lo = split(jnp.concatenate(spans, axis=0))
@@ -652,7 +644,7 @@
             for ix in range(len(middle))
         ]
         last = reached[64 * len(middle) : 64 * len(middle) + 8]
-        kept.append(jnp.where(lax.rem(tile_row, 4) == plane, last, 0.0))
+        kept.append(jnp.where(tile_row // 2 == plane, last, 0.0))
         kept.append(jnp.zeros((8, 128), F32))
         by_plane.append(jnp.concatenate(kept, axis=0))
     stacked_hi, stacked_lo = split(jnp.concatenate(by_plane, axis=1))
@@ -732,23 +724,26 @@
     summed = jnp.sum(parts[...] * weight_y, axis=1, keepdims=True)
     row = jnp.sum(jnp.where(diagonal, summed, 0.0), axis=0, keepdims=True)
 
-    def gather_sum(stage, row, count, got, ss, rs, place):
+    def gather_sum(stage, row, count, got, rs, place):
         sum_send[stage : stage + 1, :] = row
         for k in range(1, count):
             remote(
-                sum_send.at[pl.ds(stage, 1), :], got.at[pl.ds(k - 1, 1), :], ss, rs, place(k)
+                sum_send.at[pl.ds(stage, 1), :], got.at[pl.ds(k - 1, 1), :], sent, rs, place(k)
             ).start()
-        settle(ss, rs, got)
+        settle(rs, got)
         return row + jnp.sum(got[...], axis=0, keepdims=True)
 
+    sum_rows = 0
     if single:
         every = n_wall * n_span
-        row = gather_sum(
-            0, row, every, wall_got, wall_ss, wall_rs, lambda k: at(k // n_span, k % n_span)
-        )
+        row = gather_sum(0, row, every, wall_got, wall_rs, lambda k: at(k // n_span, k % n_span))
+        sum_rows = every - 1
     else:
-        row = gather_sum(0, row, n_wall, wall_got, wall_ss, wall_rs, lambda k: at(k, 0))
-        row = gather_sum(1, row, n_span, span_got, span_ss, span_rs, lambda k: at(0, k))
+        row = gather_sum(0, row, n_wall, wall_got, wall_rs, lambda k: at(k, 0))
+        row = gather_sum(1, row, n_span, span_got, span_rs[0], lambda k: at(0, k))
+        sum_rows = n_wall + n_span - 2
+    sent_rows = 2 * 2 * 64 + pull_got.shape[0] + ROUNDS * face_total + sum_rows
+    settle(sent, everything.at[pl.ds(0, sent_rows), :])
     totals = jnp.sum(jnp.where(diagonal, row, 0.0), axis=1, keepdims=True)
     m00, m01, m11, m02, m12, m22, e22 = [totals[q * 8 : q * 8 + 8, :] for q in range(7)]
     t1, t2 = shifts
@@ -839,19 +834,16 @@
             pltpu.VMEM((8, 128), F32),
             pltpu.VMEM((8, 128), F32),
             pltpu.VMEM((80, 128), F32),
-            dma,
+            pltpu.VMEM((896, length_y), F32),
             dma,
             dma,
             dma,
             dma((ROUNDS,)),
-            dma((ROUNDS,)),
-            dma,
-            dma,
-            dma,
             dma,
             pltpu.SemaphoreType.REGULAR,
             pltpu.SemaphoreType.REGULAR,
-        ],
+        ]
+        + ([] if every <= SINGLE_STAGE else [dma]),
         compiler_params=pltpu.CompilerParams(
             collective_id=0, has_side_effects=True, vmem_limit_bytes=VMEM_LIMIT
         ),

time: 21.8 us -> 21.8 us (level)
  no operation moved by 1% of the time
where the time goes in v6:
time: 21.8 us; the launch traced here: 21.6 us
  Pallas kernels  21 us (96%)
  between operations  0.64 us (3%)
    pallas_call x1, Pallas kernels, body(): pl.pallas_call(functools.partial(kernel, n_wall, n_span, sizes), out_shap...  20.2 us
    pallas_call x1, Pallas kernels, body(): pl.pallas_call(combine, out_shape=(jax.ShapeDtypeStruct(velocity_old.shap...  0.8 us

profile of v6, /device:TPU:0, one launch (start us, length us, event | category | flops | bytes accessed | tf_op | source)
XLA Modules:
  0.0 21.6 jit_solution(8651885432588217753)
XLA Ops:
  0.6 20.2 %shard_map.149 = (f32[3,3,256,128]{3,2,1,0:T(8,128)S(1)}, f32[3,8,128]{2,1,0:T(8,128)S(1)}, f32[2,512]{1,0:T(2,128)S(1)}) custom-call(f32[3,16,16,128]{3,2,1,0:T(8,128)} %vel_in.1, f32[1,16]{1,0:T(1,128)} %bitcast.7, s32[1,512]{1,0:T(1,128)} %bitcast.4, s32[1,512]{1,0:T(1,128)} %bitcast.5, f32[3,512]{1,0:T(4,128)} %coords_in.1, f32[1,512]{1,0:T(1,128)} %bitcast.6, ...), custom_call_target="tpu_custom_call" | custom-call | tf_op jit(solution)/shard_map/pallas_call | solution.py:813
  20.8 0.8 %shard_map.150 = (f32[3,16,16,128]{3,2,1,0:T(8,128)}, f32[2,512]{1,0:T(2,128)}) custom-call(f32[3,3,256,128]{3,2,1,0:T(8,128)S(1)} %get-tuple-element.5.field, f32[3,8,128]{2,1,0:T(8,128)S(1)} %get-tuple-element.6.factors, f32[2,512]{1,0:T(2,128)S(1)} %get-tuple-element.7.neumann_in), custom_call_target="tpu_custom_call" | custom-call | tf_op jit(solution)/shard_map/pallas_call | solution.py:851

commit v7 on v6

--- a/solution.py
+++ b/solution.py
@@ -329,14 +329,20 @@
     loaded("vel")
     lane = lax.broadcasted_iota(jnp.int32, (64, length_y), 1)
     groups = (length_x // 8) * count_z
+    depth = 8 * NEAR
+    strips = length_y // depth
+    packed = [jnp.zeros((64, length_y), F32)] * 2
     for index, comp in enumerate((0, 2)):
-        packed = jnp.zeros((64, length_y), F32)
         for group in range(groups):
             ex, ez = group // count_z, group % count_z
             block = vel[comp, pl.ds(ex * 8, 8), pl.ds(ez * 8, 8), :].reshape(64, length_y)
-            moved = pltpu.roll(block, (group * 32 + 16) % length_y, 1)
-            packed = jnp.where(lane // 32 == group, moved, packed)
-        near[index] = packed
+            place = index * groups + group
+            moved = pltpu.roll(block, place * depth, 1) if place else block
+            for wall_side in range(2):
+                strip = (place - wall_side) % strips
+                packed[wall_side] = jnp.where(lane // depth == strip, moved, packed[wall_side])
+    for wall_side in range(2):
+        near[wall_side] = packed[wall_side]
     def remote(src, dst, ss, rs, where):
         return pltpu.make_async_remote_copy(
             src_ref=src,
@@ -348,16 +354,19 @@
         )
 
     near_copies = []
-    for slot, dx in enumerate((1, -1)):
-        copy = remote(near, near_got.at[slot], sent, near_rs, at(dx, 0))
-        near_copies.append(copy)
+    for wall_side in range(2):
+        for slot, dx in enumerate((1, -1)):
+            target = near_got.at[wall_side, slot]
+            near_copies.append(
+                remote(near.at[wall_side], target, sent, near_rs.at[wall_side], at(dx, 0))
+            )
 
     def enter():
         pl.semaphore_wait(barrier, len(greeted))
+        if stepwise:
+            greet(step_one, across_wall)
         for copy in near_copies:
             copy.start()
-        if stepwise:
-            greet(step_one, across_wall)
 
     if stepwise:
         enter()
@@ -390,6 +399,7 @@
         size = 3 * (1 if dx and dz else length_z if dx else length_x)
         face_rows.append((sum(entry[1] for entry in face_rows), size, dx, dz))
     face_total = sum(entry[1] for entry in face_rows)
+    z_first = {entry[3]: entry[0] for entry in face_rows if entry[2] == 0}
 
     def corner(dx, dz):
         return (rows - length_z if dx == 1 else 0) + (length_z - 1 if dz == 1 else 0)
@@ -420,6 +430,10 @@
                 for first, size, dx, dz in face_rows:
                     if (2 if dx and dz else abs(dx)) != kind:
                         continue
+                    if kind == 0:
+                        swap = jnp.where(s == 0, -dz, dz)
+                        first = pl.multiple_of(jnp.where(swap == 1, z_first[1], z_first[-1]), 4)
+                        dz = swap
                     part = (turn, pl.ds(first, size), slice(None))
                     remote(
                         face_send.at[part],
@@ -494,26 +508,34 @@
     spread = jnp.concatenate(
         [jnp.where(mask, cross, 0.0) for mask in (own, from_prev, from_next)], axis=0
     )
-    n_row = lax.broadcasted_iota(jnp.int32, (length_y, points), 0)
-    within = (n_row % 32) // 8
-    layer_y = jnp.where(within < NEAR, within + (count_y - NEAR), within - NEAR)
-    wanted = (n_row // 32) * count_y + layer_y == element[...]
-    along = jnp.where(wanted, jnp.concatenate([row_y] * (length_y // 8), axis=0), 0.0)
+    half = points // 2
+    n_row = lax.broadcasted_iota(jnp.int32, (groups * depth, points), 0)
+    side_of = lax.broadcasted_iota(jnp.int32, (groups * depth, points), 1) // half
+    layer_y = (n_row % depth) // 8 + side_of * (count_y - NEAR)
+    wanted = (n_row // depth) * count_y + layer_y == element[...]
+    along = jnp.where(wanted, jnp.concatenate([row_y] * (groups * NEAR), axis=0), 0.0)
     spread = split(spread)
-
     drag = karman / jnp.log(sample_height / roughness[...])
     drag = drag * drag * (-1.0 / viscosity)
 
-    settle(near_rs, near_got)
-
     sampled = []
-    for index in range(2):
+    for wall_side in range(2):
+        settle(near_rs.at[wall_side], near_got.at[wall_side])
         sources = jnp.concatenate(
-            [near[index], near_got[0, index], near_got[1, index]], axis=0
+            [near[wall_side], near_got[wall_side, 0], near_got[wall_side, 1]], axis=0
         )
-        values = dot3(split(sources), spread, TN)
-        sampled.append(jnp.sum(values * along, axis=0, keepdims=True))
-    stream, spanwise = sampled
+        here = slice(wall_side * half, (wall_side + 1) * half)
+        values = dot3(split(sources), tuple(part[:, here] for part in spread), TN)
+        total = []
+        for index in range(2):
+            strip_rows = [
+                (place - wall_side) % strips * depth
+                for place in range(index * groups, (index + 1) * groups)
+            ]
+            own_rows = jnp.concatenate([values[k : k + depth] for k in strip_rows], axis=0)
+            total.append(jnp.sum(own_rows * along[:, here], axis=0, keepdims=True))
+        sampled.append(total)
+    stream, spanwise = [jnp.concatenate(both, axis=1) for both in zip(*sampled)]
     speed = jnp.sqrt(stream * stream + spanwise * spanwise + speed_floor)
     factor = drag * speed
     gradient = (factor * stream, factor * spanwise)
@@ -836,7 +858,7 @@
             pltpu.VMEM((80, 128), F32),
             pltpu.VMEM((896, length_y), F32),
             dma,
-            dma,
+            dma((2,)),
             dma,
             dma((ROUNDS,)),
             dma,

time: 21.8 us -> 21.6 us (level)
  no operation moved by 1% of the time
where the time goes in v7:
time: 21.6 us; the launch traced here: 21.5 us
  Pallas kernels  20.8 us (96%)
  between operations  0.64 us (3%)
    pallas_call x1, Pallas kernels, body(): pl.pallas_call(functools.partial(kernel, n_wall, n_span, sizes), out_shap...  20 us
    pallas_call x1, Pallas kernels, body(): pl.pallas_call(combine, out_shape=(jax.ShapeDtypeStruct(velocity_old.shap...  0.8 us

profile of v7, /device:TPU:0, one launch (start us, length us, event | category | flops | bytes accessed | tf_op | source)
XLA Modules:
  0.0 21.5 jit_solution(16149122596517654664)
XLA Ops:
  0.6 20.0 %shard_map.149 = (f32[3,3,256,128]{3,2,1,0:T(8,128)S(1)}, f32[3,8,128]{2,1,0:T(8,128)S(1)}, f32[2,512]{1,0:T(2,128)S(1)}) custom-call(f32[3,16,16,128]{3,2,1,0:T(8,128)} %vel_in.1, f32[1,16]{1,0:T(1,128)} %bitcast.7, s32[1,512]{1,0:T(1,128)} %bitcast.4, s32[1,512]{1,0:T(1,128)} %bitcast.5, f32[3,512]{1,0:T(4,128)} %coords_in.1, f32[1,512]{1,0:T(1,128)} %bitcast.6, ...), custom_call_target="tpu_custom_call" | custom-call | tf_op jit(solution)/shard_map/pallas_call | solution.py:835
  20.7 0.8 %shard_map.150 = (f32[3,16,16,128]{3,2,1,0:T(8,128)}, f32[2,512]{1,0:T(2,128)}) custom-call(f32[3,3,256,128]{3,2,1,0:T(8,128)S(1)} %get-tuple-element.5.field, f32[3,8,128]{2,1,0:T(8,128)S(1)} %get-tuple-element.6.factors, f32[2,512]{1,0:T(2,128)S(1)} %get-tuple-element.7.neumann_in), custom_call_target="tpu_custom_call" | custom-call | tf_op jit(solution)/shard_map/pallas_call | solution.py:873

commit v8 on v7

--- a/solution.py
+++ b/solution.py
@@ -137,10 +137,19 @@
     inner_z = face_weights(length_z, True)
     outer_x = face_weights(length_x, False)
     outer_z = face_weights(length_z, False)
-    columns = np.stack(
-        [assembled, mass_plane, np.kron(outer_x, outer_z), np.kron(inner_x, inner_z)]
-    )
-    columns = columns[:, :, None] * np.ones(length_y)[None, None]
+    steps_x, steps_z = np.arange(length_x), np.arange(length_z)
+    fringe = np.concatenate(
+        [
+            steps_x * length_z + length_z - 1,
+            steps_x * length_z,
+            (length_x - 1) * length_z + steps_z,
+            steps_z,
+        ]
+    )
+    outer, inner = np.kron(outer_x, outer_z), np.kron(inner_x, inner_z)
+    columns = np.concatenate([assembled, mass_plane, mass_plane[fringe], outer, inner])
+    columns = columns.reshape(-1, 1) * np.ones(length_y)[None]
+    plane = np.concatenate([plane, plane[fringe]], axis=0)
     reach = 2 * REACH + 1
 
     def words(length, mass, stiff, extra):
@@ -245,7 +254,6 @@
     load_sem,
     near,
     near_got,
-    local,
     face_send,
     face_got,
     parts,
@@ -274,6 +282,13 @@
     def at(dx, dz):
         return (lax.rem(w + (dx + n_wall), n_wall), lax.rem(s + (dz + n_span), n_span))
 
+    edges = 2 * (length_x + length_z)
+    early, late = pl.ds(0, 2 * rows + edges), pl.ds(2 * rows + edges, 2 * rows)
+
+    def column(index):
+        first = index * rows + (edges if index > 1 else 0)
+        return columns[first : first + rows, :]
+
     loads = {
         name: pltpu.make_async_copy(source, target, load_sem.at[index])
         for index, (name, source, target) in enumerate(
@@ -281,7 +296,7 @@
                 ("vel", vel_in, vel),
                 ("heights", heights_in, heights),
                 ("lines", lines_in, lines),
-                ("scale", columns_in.at[pl.ds(0, 2)], columns.at[pl.ds(0, 2)]),
+                ("scale", columns_in.at[early], columns.at[early]),
                 ("plane", plane_in, sheet),
                 ("coords", coords_in, coords),
                 ("owner", owner_in, owner),
@@ -289,7 +304,7 @@
                 ("roughness", roughness_in, roughness),
                 ("along_x", along_x_in, along_x),
                 ("along_z", along_z_in, along_z),
-                ("weights", columns_in.at[pl.ds(2, 2)], columns.at[pl.ds(2, 2)]),
+                ("weights", columns_in.at[late], columns.at[late]),
             )
         )
     }
@@ -390,7 +405,7 @@
     shifts = (0.15 * bound, 0.85 * bound)
 
     mass_row = jnp.sum(lines_mass, axis=0, keepdims=True)
-    scale = columns[0] * mass_row
+    scale = column(0) * mass_row
     for c in range(3):
         field[0, c] = vel[c].reshape(rows, length_y) * scale
 
@@ -414,11 +429,19 @@
             rows_of = pl.ds(length_z - 1 if dz == 1 else 0, length_x, stride=length_z)
         return pl.ds(first, size), rows_of
 
-    def send_faces(turn):
+    def send_faces(turn, fringe):
         for c in range(3):
-            for slot, (_, _, dx, dz) in enumerate(face_rows):
-                packed_rows, rows_of = face_part(slot, c, dx, dz)
-                face_send[turn, packed_rows, :] = local[turn, c, rows_of, :]
+            for slot, (first, size, dx, dz) in enumerate(face_rows):
+                size //= 3
+                if dx and dz:
+                    begin = 2 * length_x + (length_z if dx == -1 else 0)
+                    begin += length_z - 1 if dz == 1 else 0
+                elif dx:
+                    begin = 2 * length_x + (length_z if dx == -1 else 0)
+                else:
+                    begin = length_x if dz == -1 else 0
+                rows_here = slice(first + c * size, first + (c + 1) * size)
+                face_send[turn, rows_here, :] = fringe[c][begin : begin + size]
         first_turn = turn == 0 and stepwise
         if turn == 0 and not stepwise:
             enter()
@@ -460,39 +483,55 @@
             product, axis=0, keepdims=True
         )
 
-    def operate(source, target):
-        highs, lows = zip(*[split(field[source, c]) for c in range(3)])
-        along_y = jnp.dot(
-            jnp.concatenate(
-                [jnp.concatenate([high, low], axis=1) for high, low in zip(highs, lows)], axis=0
-            ),
-            lines_packed,
-            preferred_element_type=F32,
-        )
-        across = jnp.dot(
-            sheet[0], jnp.concatenate(highs + lows, axis=1), preferred_element_type=F32
-        )
-        across_low = jnp.dot(sheet[1], jnp.concatenate(highs, axis=1), preferred_element_type=F32)
+    def operate(turn):
+        highs, lows = zip(*[split(field[turn, c]) for c in range(3)])
+        packed = [jnp.concatenate(pair, axis=1) for pair in zip(highs, lows)]
+        wide = jnp.concatenate(highs + lows, axis=1)
+        wide_high = jnp.concatenate(highs, axis=1)
+
+        def image(first, count, lines_of, weight):
+            along_y = jnp.dot(
+                jnp.concatenate(lines_of, axis=0), lines_packed, preferred_element_type=F32
+            )
+            part = slice(first, first + count)
+            across = jnp.dot(sheet[0, part], wide, preferred_element_type=F32)
+            across_low = jnp.dot(sheet[1, part], wide_high, preferred_element_type=F32)
+            results = []
+            for c in range(3):
+                here = slice(c * length_y, (c + 1) * length_y)
+                also = slice((3 + c) * length_y, (4 + c) * length_y)
+                flat = across[:, here] + (across[:, also] + across_low[:, here])
+                tall = along_y[c * count : (c + 1) * count]
+                tall = tall[:, :length_y] + tall[:, length_y:]
+                results.append(flat * mass_row + tall * weight)
+            return results
+
+        lines_of = []
         for c in range(3):
-            here = slice(c * length_y, (c + 1) * length_y)
-            also = slice((3 + c) * length_y, (4 + c) * length_y)
-            flat = across[:, here] + (across[:, also] + across_low[:, here])
-            tall = along_y[c * rows : (c + 1) * rows]
-            tall = tall[:, :length_y] + tall[:, length_y:]
-            local[target, c] = flat * mass_row + tall * columns[1]
+            value = jnp.concatenate(
+                [
+                    field[turn, c, pl.ds(length_z - 1, length_x, stride=length_z), :],
+                    field[turn, c, pl.ds(0, length_x, stride=length_z), :],
+                    field[turn, c, pl.ds(rows - length_z, length_z), :],
+                    field[turn, c, pl.ds(0, length_z), :],
+                ],
+                axis=0,
+            )
+            lines_of.append(jnp.concatenate(split(value), axis=1))
+        weight = columns[2 * rows : 2 * rows + edges, :]
+        send_faces(turn, image(rows, edges, lines_of, weight))
+        for c, value in enumerate(image(0, rows, packed, column(1))):
+            field[turn + 1, c] = value
 
     slots = {(0, 0): 0, (0, 1): 1, (1, 1): 2, (0, 2): 3, (1, 2): 4, (2, 2): 5}
 
     def inner_products(newest):
         for c in range(3):
-            weighted = field[newest, c] * columns[2]
+            weighted = field[newest, c] * column(2)
             for other in range(newest + 1):
                 inner(slots[(other, newest)], c, weighted * field[other, c])
 
-    operate(0, 0)
-    send_faces(0)
-    for c in range(3):
-        field[1, c] = local[0, c]
+    operate(0)
     parts[...] = jnp.zeros_like(parts)
 
     loaded("coords", "owner", "element", "roughness")
@@ -589,10 +628,7 @@
         ).start()
 
     add_faces(0)
-    operate(1, 1)
-    send_faces(1)
-    for c in range(3):
-        field[2, c] = local[1, c]
+    operate(1)
     loaded("along_x", "along_z", "weights")
     lines_rows = jnp.concatenate([lines_mass, lines_stiff], axis=1)
     ends = [lines_rows[0:1], lines_rows[length_y - 1 : length_y]]
@@ -723,17 +759,17 @@
         jnp.concatenate(highs, axis=0), lines_packed[:length_y], preferred_element_type=F32
     )
     wide = jnp.concatenate(highs, axis=1)
-    across = jnp.dot(sheet[0], wide, preferred_element_type=F32)
-    across_low = jnp.dot(sheet[1], wide, preferred_element_type=F32)
+    across = jnp.dot(sheet[0, :rows], wide, preferred_element_type=F32)
+    across_low = jnp.dot(sheet[1, :rows], wide, preferred_element_type=F32)
     inner_products(2)
     for c in range(3):
         here = slice(c * length_y, (c + 1) * length_y)
         tall = along_y[c * rows : (c + 1) * rows]
         tall = tall[:, :length_y] + tall[:, length_y:]
-        image = (across[:, here] + across_low[:, here]) * mass_row + tall * columns[1]
+        image = (across[:, here] + across_low[:, here]) * mass_row + tall * column(1)
         value = field[2, c]
         partner = value + (value - highs[c].astype(F32))
-        inner(6, c, partner * columns[3] * image)
+        inner(6, c, partner * column(3) * image)
 
     total_rows = parts.shape[0]
     r_iota = lax.broadcasted_iota(jnp.int32, (total_rows, 128), 0)
@@ -846,7 +882,6 @@
             dma((12,)),
             pltpu.VMEM((2, 64, length_y), F32),
             pltpu.VMEM((2, 2, 64, length_y), F32),
-            pltpu.VMEM((ROUNDS, 3, rows, length_y), F32),
             pltpu.VMEM((ROUNDS, faces, length_y), F32),
             pltpu.VMEM((ROUNDS, faces, length_y), F32),
             pltpu.VMEM((56, length_y), F32),

time: 21.6 us -> 21.6 us (level)
  no operation moved by 1% of the time
where the time goes in v8:
time: 21.6 us; the launch traced here: 21.5 us
  Pallas kernels  20.8 us (96%)
  between operations  0.64 us (3%)
    pallas_call x1, Pallas kernels, body(): pl.pallas_call(functools.partial(kernel, n_wall, n_span, sizes), out_shap...  20 us
    pallas_call x1, Pallas kernels, body(): pl.pallas_call(combine, out_shape=(jax.ShapeDtypeStruct(velocity_old.shap...  0.8 us

profile of v8, /device:TPU:0, one launch (start us, length us, event | category | flops | bytes accessed | tf_op | source)
XLA Modules:
  0.0 21.5 jit_solution(6724024991505242961)
XLA Ops:
  0.6 20.0 %shard_map.149 = (f32[3,3,256,128]{3,2,1,0:T(8,128)S(1)}, f32[3,8,128]{2,1,0:T(8,128)S(1)}, f32[2,512]{1,0:T(2,128)S(1)}) custom-call(f32[3,16,16,128]{3,2,1,0:T(8,128)} %vel_in.1, f32[1,16]{1,0:T(1,128)} %bitcast.7, s32[1,512]{1,0:T(1,128)} %bitcast.4, s32[1,512]{1,0:T(1,128)} %bitcast.5, f32[3,512]{1,0:T(4,128)} %coords_in.1, f32[1,512]{1,0:T(1,128)} %bitcast.6, ...), custom_call_target="tpu_custom_call" | custom-call | tf_op jit(solution)/shard_map/pallas_call | solution.py:871
  20.7 0.8 %shard_map.150 = (f32[3,16,16,128]{3,2,1,0:T(8,128)}, f32[2,512]{1,0:T(2,128)}) custom-call(f32[3,3,256,128]{3,2,1,0:T(8,128)S(1)} %get-tuple-element.5.field, f32[3,8,128]{2,1,0:T(8,128)S(1)} %get-tuple-element.6.factors, f32[2,512]{1,0:T(2,128)S(1)} %get-tuple-element.7.neumann_in), custom_call_target="tpu_custom_call" | custom-call | tf_op jit(solution)/shard_map/pallas_call | solution.py:908

commit v9 on v8

--- a/solution.py
+++ b/solution.py
@@ -279,8 +279,11 @@
     w = lax.axis_index("wall")
     s = lax.axis_index("span")
 
+    def turned(place, count):
+        return place & (count - 1) if count & (count - 1) == 0 else lax.rem(place, count)
+
     def at(dx, dz):
-        return (lax.rem(w + (dx + n_wall), n_wall), lax.rem(s + (dz + n_span), n_span))
+        return (turned(w + (dx + n_wall), n_wall), turned(s + (dz + n_span), n_span))
 
     edges = 2 * (length_x + length_z)
     early, late = pl.ds(0, 2 * rows + edges), pl.ds(2 * rows + edges, 2 * rows)
@@ -598,9 +601,9 @@
         spread_rows = pltpu.roll(spread_rows, (8 - tile) % 8, 0)
         bundle = jnp.where(block_of == tile, spread_rows, bundle)
         for end in range(2):
-            turned = pltpu.roll(part, 7 * (1 - end), 1, stride=length_z - 1, stride_axis=0)
+            slanted = pltpu.roll(part, 7 * (1 - end), 1, stride=length_z - 1, stride_axis=0)
             wanted_lane = tile * length_z + 8 * end + 7 - tile_row
-            fringe = jnp.where(tile_lane == wanted_lane, turned, fringe)
+            fringe = jnp.where(tile_lane == wanted_lane, slanted, fringe)
     pull_send[...] = bundle
     edge_send[0:1, :] = jnp.sum(fringe, axis=0, keepdims=True)
     edge_send[1:2, :] = jnp.where(block_of[0:1] % 2 == 0, bundle[0:1], bundle[1:2])
@@ -661,6 +664,22 @@
     low_half = tile_lane & 8 == 0
     low_rows = tile_row & 1 == 0
     diagonal_of = (tile_lane + tile_row) & 7
+
+    def halves(value):
+        return split(value)
+
+    def both_tiles(pair, mask_of):
+        masks = [jnp.where(mask_of(tile), 1.0, 0.0) for tile in (2 * pair, 2 * pair + 1)]
+        return jnp.concatenate(masks, axis=0).astype(BF16)
+
+    block_masks = [both_tiles(pair, lambda tile: block_of == tile) for pair in range(tiles // 2)]
+    end_masks = [
+        both_tiles(
+            pair,
+            lambda tile: jnp.logical_and(block_of == tile, diagonal_of == (7 - tile) % 8),
+        )
+        for pair in range(tiles // 2)
+    ]
     settle(pull_rs, pull_got)
 
     def edge(dx, dz):
@@ -670,15 +689,20 @@
         return jnp.where(low_half, edge(dx, REACH), edge(dx, -REACH))
 
     middle = range(-REACH + 1, REACH)
-    spans = []
+
+    def doubled(part):
+        return [jnp.concatenate([half, half], axis=0) for half in (part[0], part[1])]
+
+    spans = ([], [])
     for dx in middle:
-        ends = both_ends(dx)
         parts_z = [bundle if (dx, dz) == (0, 0) else pull_got[pull_rows[(dx, dz)], :] for dz in middle]
-        for tile in range(tiles):
-            pieces = [jnp.where(block_of == tile, part, 0.0) for part in parts_z]
-            kept = jnp.logical_and(block_of == tile, diagonal_of == (7 - tile) % 8)
-            pieces.append(jnp.where(kept, ends, 0.0))
-            spans.append(jnp.concatenate(pieces, axis=1))
+        pairs = [doubled(halves(part)) for part in parts_z]
+        ends = doubled(halves(both_ends(dx)))
+        for pair in range(tiles // 2):
+            for out, which in zip(spans, range(2)):
+                pieces = [part[which] * block_masks[pair] for part in pairs]
+                pieces.append(ends[which] * end_masks[pair])
+                out.append(jnp.concatenate(pieces, axis=1))
     pieces = [
         jnp.where(block_of == tile_row, jnp.where(low_rows, edge(REACH, dz), edge(-REACH, dz)), 0.0)
         for dz in middle
@@ -688,9 +712,10 @@
     )
     ends = jnp.where(low_rows, both_ends(REACH), both_ends(-REACH))
     pieces.append(jnp.where(kept, ends, 0.0))
-    spans.append(jnp.concatenate(pieces, axis=1))
-    spans.append(jnp.zeros((8, 512), F32))
-    spans_hi, spans_lo = split(jnp.concatenate(spans, axis=0))
+    last = jnp.concatenate([jnp.concatenate(pieces, axis=1), jnp.zeros((8, 512), F32)], axis=0)
+    for out, half in zip(spans, split(last)):
+        out.append(half)
+    spans_hi, spans_lo = [jnp.concatenate(out, axis=0) for out in spans]
     reached = jnp.dot(spans_hi, along_z[...], preferred_element_type=F32)
     reached = (reached[:, :128] + reached[:, 128:]) + jnp.dot(
         spans_lo, along_z[:, :128], preferred_element_type=F32
@@ -784,7 +809,15 @@
 
     def gather_sum(stage, row, count, got, rs, place):
         sum_send[stage : stage + 1, :] = row
-        for k in range(1, count):
+        def ring(place, size):
+            return min(place % size, -place % size)
+
+        def reach_of(k):
+            if count != n_wall * n_span:
+                return ring(k, count)
+            return ring(k // n_span, n_wall) + ring(k % n_span, n_span)
+
+        for k in sorted(range(1, count), key=reach_of, reverse=True):
             remote(
                 sum_send.at[pl.ds(stage, 1), :], got.at[pl.ds(k - 1, 1), :], sent, rs, place(k)
             ).start()

time: 21.6 us -> 21.6 us (level)
  no operation moved by 1% of the time
where the time goes in v9:
time: 21.6 us; the launch traced here: 21.5 us
  Pallas kernels  20.8 us (96%)
  between operations  0.64 us (3%)
    pallas_call x1, Pallas kernels, body(): pl.pallas_call(functools.partial(kernel, n_wall, n_span, sizes), out_shap...  20 us
    pallas_call x1, Pallas kernels, body(): pl.pallas_call(combine, out_shape=(jax.ShapeDtypeStruct(velocity_old.shap...  0.8 us

profile of v9, /device:TPU:0, one launch (start us, length us, event | category | flops | bytes accessed | tf_op | source)
XLA Modules:
  0.0 21.5 jit_solution(15445276872848505967)
XLA Ops:
  0.6 20.0 %shard_map.149 = (f32[3,3,256,128]{3,2,1,0:T(8,128)S(1)}, f32[3,8,128]{2,1,0:T(8,128)S(1)}, f32[2,512]{1,0:T(2,128)S(1)}) custom-call(f32[3,16,16,128]{3,2,1,0:T(8,128)} %vel_in.1, f32[1,16]{1,0:T(1,128)} %bitcast.7, s32[1,512]{1,0:T(1,128)} %bitcast.4, s32[1,512]{1,0:T(1,128)} %bitcast.5, f32[3,512]{1,0:T(4,128)} %coords_in.1, f32[1,512]{1,0:T(1,128)} %bitcast.6, ...), custom_call_target="tpu_custom_call" | custom-call | tf_op jit(solution)/shard_map/pallas_call | solution.py:904
  20.7 0.8 %shard_map.150 = (f32[3,16,16,128]{3,2,1,0:T(8,128)}, f32[2,512]{1,0:T(2,128)}) custom-call(f32[3,3,256,128]{3,2,1,0:T(8,128)S(1)} %get-tuple-element.5.field, f32[3,8,128]{2,1,0:T(8,128)S(1)} %get-tuple-element.6.factors, f32[2,512]{1,0:T(2,128)S(1)} %get-tuple-element.7.neumann_in), custom_call_target="tpu_custom_call" | custom-call | tf_op jit(solution)/shard_map/pallas_call | solution.py:941

commit v10 on v9

--- a/solution.py
+++ b/solution.py
@@ -1,4 +1,5 @@
 import functools
+import math
 
 import jax
 import jax.numpy as jnp
@@ -285,39 +286,7 @@
     def at(dx, dz):
         return (turned(w + (dx + n_wall), n_wall), turned(s + (dz + n_span), n_span))
 
-    edges = 2 * (length_x + length_z)
-    early, late = pl.ds(0, 2 * rows + edges), pl.ds(2 * rows + edges, 2 * rows)
-
-    def column(index):
-        first = index * rows + (edges if index > 1 else 0)
-        return columns[first : first + rows, :]
-
-    loads = {
-        name: pltpu.make_async_copy(source, target, load_sem.at[index])
-        for index, (name, source, target) in enumerate(
-            (
-                ("vel", vel_in, vel),
-                ("heights", heights_in, heights),
-                ("lines", lines_in, lines),
-                ("scale", columns_in.at[early], columns.at[early]),
-                ("plane", plane_in, sheet),
-                ("coords", coords_in, coords),
-                ("owner", owner_in, owner),
-                ("element", element_in, element),
-                ("roughness", roughness_in, roughness),
-                ("along_x", along_x_in, along_x),
-                ("along_z", along_z_in, along_z),
-                ("weights", columns_in.at[late], columns.at[late]),
-            )
-        )
-    }
-    for load in loads.values():
-        load.start()
-
-    def loaded(*names):
-        for name in names:
-            loads[name].wait()
-
+    pltpu.make_async_copy(vel_in, vel, load_sem.at[0]).start()
     single = n_wall * n_span <= SINGLE_STAGE
     stepwise = single and 3 <= n_wall <= 4 * REACH and 3 <= n_span <= 4 * REACH
     across_wall = ((1, 0), (-1, 0))
@@ -343,6 +312,42 @@
             pl.semaphore_signal(semaphore, inc=1, device_id=at(dx, dz), device_id_type=MESH)
 
     greet(barrier, greeted)
+
+    edges = 2 * (length_x + length_z)
+    early, late = pl.ds(0, 2 * rows + edges), pl.ds(2 * rows + edges, 2 * rows)
+
+    def column(index):
+        first = index * rows + (edges if index > 1 else 0)
+        return columns[first : first + rows, :]
+
+    loads = {
+        "vel": [(vel_in, vel)],
+        "heights": [(heights_in, heights)],
+        "operator": [
+            (lines_in, lines),
+            (columns_in.at[early], columns.at[early]),
+            (plane_in, sheet),
+        ],
+        "coords": [(coords_in, coords)],
+        "points": [(owner_in, owner), (element_in, element), (roughness_in, roughness)],
+        "words": [
+            (along_x_in, along_x),
+            (along_z_in, along_z),
+            (columns_in.at[late], columns.at[late]),
+        ],
+    }
+    for index, group in list(enumerate(loads.values()))[1:]:
+        for source, target in group:
+            pltpu.make_async_copy(source, target, load_sem.at[index]).start()
+
+    def loaded(*names):
+        for name in names:
+            index, group = list(loads).index(name), loads[name]
+            whole = group[0][1]
+            if len(group) > 1:
+                size = sum(math.prod(ref.shape) * ref.dtype.itemsize for _, ref in group)
+                whole = everything.at[pl.ds(0, size // (4 * length_y)), :]
+            pltpu.make_async_copy(whole, whole, load_sem.at[index]).wait()
 
     loaded("vel")
     lane = lax.broadcasted_iota(jnp.int32, (64, length_y), 1)
@@ -388,7 +393,7 @@
 
     if stepwise:
         enter()
-    loaded("heights", "lines", "scale", "plane")
+    loaded("heights", "operator")
 
     layer_of = lax.broadcasted_iota(jnp.int32, (length_y, count_y), 0) // 8
     layer = lax.broadcasted_iota(jnp.int32, (length_y, count_y), 1)
@@ -537,7 +542,7 @@
     operate(0)
     parts[...] = jnp.zeros_like(parts)
 
-    loaded("coords", "owner", "element", "roughness")
+    loaded("coords", "points")
     points = owner.shape[1]
     row_x = lagrange_rows(coords[0:1, :])
     row_z = lagrange_rows(coords[1:2, :])
@@ -632,7 +637,7 @@
 
     add_faces(0)
     operate(1)
-    loaded("along_x", "along_z", "weights")
+    loaded("words")
     lines_rows = jnp.concatenate([lines_mass, lines_stiff], axis=1)
     ends = [lines_rows[0:1], lines_rows[length_y - 1 : length_y]]
     once = [(end[:, :length_y], end[:, length_y:]) for end in ends]
@@ -732,7 +737,7 @@
         by_plane.append(jnp.concatenate(kept, axis=0))
     stacked_hi, stacked_lo = split(jnp.concatenate(by_plane, axis=1))
     both_ways = jnp.dot(
-        along_x[...],
+        along_x[:, : 3 * stacked_hi.shape[0]],
         jnp.concatenate([stacked_hi, stacked_lo, stacked_hi], axis=0),
         preferred_element_type=F32,
     )
@@ -897,7 +902,7 @@
         jnp.stack(split_np(plane)),
         jnp.asarray(lines, F32),
         jnp.asarray(columns, F32),
-        jnp.concatenate([along_x_hi, along_x_hi, along_x_lo], axis=1),
+        jnp.pad(jnp.concatenate([along_x_hi, along_x_hi, along_x_lo], axis=1), ((0, 0), (0, 64))),
         jnp.concatenate(split_np(along_z), axis=1),
     )
     dma = pltpu.SemaphoreType.DMA
@@ -912,7 +917,7 @@
         out_specs=(vmem, vmem, vmem),
         scratch_shapes=[pltpu.VMEM(value.shape, value.dtype) for value in operands]
         + [
-            dma((12,)),
+            dma((6,)),
             pltpu.VMEM((2, 64, length_y), F32),
             pltpu.VMEM((2, 2, 64, length_y), F32),
             pltpu.VMEM((ROUNDS, faces, length_y), F32),
@@ -924,7 +929,7 @@
             pltpu.VMEM((8, 128), F32),
             pltpu.VMEM((8, 128), F32),
             pltpu.VMEM((80, 128), F32),
-            pltpu.VMEM((896, length_y), F32),
+            pltpu.VMEM((1536, length_y), F32),
             dma,
             dma((2,)),
             dma,

time: 21.6 us -> 21.6 us (level)
  no operation moved by 1% of the time
where the time goes in v10:
time: 21.6 us; the launch traced here: 21.4 us
  Pallas kernels  20.8 us (96%)
  between operations  0.64 us (3%)
    pallas_call x1, Pallas kernels, body(): pl.pallas_call(functools.partial(kernel, n_wall, n_span, sizes), out_shap...  20 us
    pallas_call x1, Pallas kernels, body(): pl.pallas_call(combine, out_shape=(jax.ShapeDtypeStruct(velocity_old.shap...  0.8 us

profile of v10, /device:TPU:0, one launch (start us, length us, event | category | flops | bytes accessed | tf_op | source)
XLA Modules:
  0.0 21.4 jit_solution(3906232872989771340)
XLA Ops:
  0.6 20.0 %shard_map.149 = (f32[3,3,256,128]{3,2,1,0:T(8,128)S(1)}, f32[3,8,128]{2,1,0:T(8,128)S(1)}, f32[2,512]{1,0:T(2,128)S(1)}) custom-call(f32[3,16,16,128]{3,2,1,0:T(8,128)} %vel_in.1, f32[1,16]{1,0:T(1,128)} %bitcast.7, s32[1,512]{1,0:T(1,128)} %bitcast.4, s32[1,512]{1,0:T(1,128)} %bitcast.5, f32[3,512]{1,0:T(4,128)} %coords_in.1, f32[1,512]{1,0:T(1,128)} %bitcast.6, ...), custom_call_target="tpu_custom_call" | custom-call | tf_op jit(solution)/shard_map/pallas_call | solution.py:909
  20.6 0.8 %shard_map.150 = (f32[3,16,16,128]{3,2,1,0:T(8,128)}, f32[2,512]{1,0:T(2,128)}) custom-call(f32[3,3,256,128]{3,2,1,0:T(8,128)S(1)} %get-tuple-element.5.field, f32[3,8,128]{2,1,0:T(8,128)S(1)} %get-tuple-element.6.factors, f32[2,512]{1,0:T(2,128)S(1)} %get-tuple-element.7.neumann_in), custom_call_target="tpu_custom_call" | custom-call | tf_op jit(solution)/shard_map/pallas_call | solution.py:946

commit v11 on v10

--- a/solution.py
+++ b/solution.py
@@ -864,19 +864,20 @@
 
 
 def combine(field, factors, neumann_in, out, neumann, stage, sems):
-    small = pltpu.make_async_copy(neumann_in, neumann, sems.at[3])
+    small = pltpu.make_async_copy(neumann_in, neumann, sems.at[1])
     small.start()
-    copies = []
+    length_x, length_z, length_y = stage.shape[1:]
+    half = length_x // 2
     for c in range(3):
-        result = factors[0, c : c + 1] * field[0, c]
-        for level in range(1, 3):
-            result += factors[level, c : c + 1] * field[level, c]
-        stage[c] = result.reshape(stage.shape[1:])
-        copy = pltpu.make_async_copy(stage.at[c], out.at[c], sems.at[c])
-        copy.start()
-        copies.append(copy)
-    for copy in copies:
-        copy.wait()
+        for first in (0, half):
+            here = slice(first * length_z, (first + half) * length_z)
+            result = factors[0, c : c + 1] * field[0, c, here]
+            for level in range(1, 3):
+                result += factors[level, c : c + 1] * field[level, c, here]
+            stage[c, first : first + half] = result.reshape(half, length_z, length_y)
+            part = (c, pl.ds(first, half))
+            pltpu.make_async_copy(stage.at[part], out.at[part], sems.at[0]).start()
+    pltpu.make_async_copy(stage, out, sems.at[0]).wait()
     small.wait()
 
 
@@ -951,7 +952,7 @@
         ),
         in_specs=[vmem] * 3,
         out_specs=(hbm, hbm),
-        scratch_shapes=[pltpu.VMEM(velocity_old.shape, F32), dma((4,))],
+        scratch_shapes=[pltpu.VMEM(velocity_old.shape, F32), dma((2,))],
         compiler_params=pltpu.CompilerParams(vmem_limit_bytes=VMEM_LIMIT),
     )(field, factors, neumann)
 

time: 21.6 us -> 21.5 us (level)
  no operation moved by 1% of the time
where the time goes in v11:
time: 21.5 us; the launch traced here: 21.4 us
  Pallas kernels  20.7 us (96%)
  between operations  0.64 us (3%)
    pallas_call x1, Pallas kernels, body(): pl.pallas_call(functools.partial(kernel, n_wall, n_span, sizes), out_shap...  20 us
    pallas_call x1, Pallas kernels, body(): pl.pallas_call(combine, out_shape=(jax.ShapeDtypeStruct(velocity_old.shap...  0.77 us

profile of v11, /device:TPU:0, one launch (start us, length us, event | category | flops | bytes accessed | tf_op | source)
XLA Modules:
  0.0 21.4 jit_solution(14659936326155889282)
XLA Ops:
  0.6 20.0 %shard_map.149 = (f32[3,3,256,128]{3,2,1,0:T(8,128)S(1)}, f32[3,8,128]{2,1,0:T(8,128)S(1)}, f32[2,512]{1,0:T(2,128)S(1)}) custom-call(f32[3,16,16,128]{3,2,1,0:T(8,128)} %vel_in.1, f32[1,16]{1,0:T(1,128)} %bitcast.7, s32[1,512]{1,0:T(1,128)} %bitcast.4, s32[1,512]{1,0:T(1,128)} %bitcast.5, f32[3,512]{1,0:T(4,128)} %coords_in.1, f32[1,512]{1,0:T(1,128)} %bitcast.6, ...), custom_call_target="tpu_custom_call" | custom-call | tf_op jit(solution)/shard_map/pallas_call | solution.py:910
  20.6 0.8 %shard_map.150 = (f32[3,16,16,128]{3,2,1,0:T(8,128)}, f32[2,512]{1,0:T(2,128)}) custom-call(f32[3,3,256,128]{3,2,1,0:T(8,128)S(1)} %get-tuple-element.5.field, f32[3,8,128]{2,1,0:T(8,128)S(1)} %get-tuple-element.6.factors, f32[2,512]{1,0:T(2,128)S(1)} %get-tuple-element.7.neumann_in), custom_call_target="tpu_custom_call" | custom-call | tf_op jit(solution)/shard_map/pallas_call | solution.py:947
